TPU v7x, 32 devices: a whole 2x2x4 slice. The times are simulated.
32 devices in a mesh: inter: 16 (over z, y, core), intra: 2 (over x).
Axes of the slice: x: 2, y: 2, z: 4, core: 2. Of those that a mesh axis runs over, the one named last changes fastest.
Arguments:
- hidden_in: bfloat16 [16, 256, 4096], P('inter', 'intra'), may hold values from -120 to 120, as said below
- norm_gain: bfloat16 [4096], P(('inter', 'intra')), may hold values from 0.5 to 2, as said below
- qkv_weight: bfloat16 [4096, 768], P(('inter', 'intra')), may hold values from -0.09375 to 0.09375
- attn_cotangent: bfloat16 [16, 256, 512], P('inter', 'intra'), may hold values from -6 to 6
Outputs:
- attn: bfloat16 [16, 256, 512], P('inter', 'intra')
- grad_in: bfloat16 [16, 256, 4096], P('inter', 'intra')
- weight_grad: float32 [4096, 768], P(('intra', 'inter'))
- gain_grad: float32 [4096], P(('intra', 'inter'))
Inputs may be any that keep to these rules, and one draw needn't show every extreme that they name: `hidden_in`: activations with spread row and feature scales. `norm_gain`: positive gains.
All inputs are finite; a program needn't handle non-finite values.
Results may differ from a plain program's by a relative error of at most 0.015.
Values may be sent and summed in bfloat16 or wider, within the bound.
A program may use at most 64 MiB of HBM per device.

v0:
```python
import functools
import jax
import jax.numpy as jnp
import numpy as np
from jax import lax
from jax.experimental import pallas as pl
from jax.experimental.pallas import tpu as pltpu
from jax.sharding import PartitionSpec as P

HD = 128
HEADS = 4


eps_norm = 1e-05
rope_base = 500000.0


def rope_tables(positions, head_size):
    half_size = head_size // 2
    freqs = rope_base ** (-jnp.arange(half_size, dtype=jnp.float32) / half_size)
    angles = positions.astype(jnp.float32)[:, None] * freqs[None, :]
    return (jnp.cos(angles), jnp.sin(angles))


def rotate(values_in, cosine, sine):
    half_size = values_in.shape[-1] // 2
    first, second = (values_in[..., :half_size], values_in[..., half_size:])
    return jnp.concatenate(
        [first * cosine - second * sine, second * cosine + first * sine], axis=-1
    )


def unrotate(grad_out, cosine, sine):
    half_size = grad_out.shape[-1] // 2
    first, second = (grad_out[..., :half_size], grad_out[..., half_size:])
    return jnp.concatenate(
        [first * cosine + second * sine, second * cosine - first * sine], axis=-1
    )


def forward_fold(query_rows, row_pos):

    def forward_advance(carry, piece, start):
        row_top, row_total, weighted = carry
        key_part, value_part = piece
        scores = jnp.einsum("qd,kd->qk", query_rows, key_part, preferred_element_type=jnp.float32)
        key_pos = jnp.arange(key_part.shape[0], dtype=jnp.int32)
        allowed = key_pos[None, :] <= row_pos[:, None]
        scores = jnp.where(allowed, scores, -1e30)
        new_top = jnp.maximum(row_top, jnp.max(scores, axis=1))
        numbers = jnp.where(allowed, jnp.exp(scores - new_top[:, None]), 0.0)
        row_total = jnp.sum(numbers, axis=1)
        weighted = jnp.dot(
            numbers,
            value_part.astype(jnp.float32),
            precision=lax.Precision.HIGHEST,
            preferred_element_type=jnp.float32,
        )
        return (new_top, row_total, weighted)

    return forward_advance


def query_grad_fold(query_rows, row_pos, grad_flat, log_total, row_delta):

    def query_advance(grad_query, piece, start):
        key_part, value_part = piece
        scores = jnp.einsum("qd,kd->qk", query_rows, key_part, preferred_element_type=jnp.float32)
        key_pos = jnp.arange(key_part.shape[0], dtype=jnp.int32)
        allowed = key_pos[None, :] <= row_pos[:, None]
        probs = jnp.where(
            allowed, jnp.exp(jnp.where(allowed, scores, -1e30) - log_total[:, None]), 0.0
        )
        grad_probs = jnp.einsum(
            "qd,kd->qk", grad_flat, value_part, preferred_element_type=jnp.float32
        )
        grad_scores = (probs * (grad_probs - row_delta[:, None])).astype(jnp.bfloat16)
        return jnp.dot(grad_scores, key_part, preferred_element_type=jnp.float32)

    return query_advance


def key_grad_fold(key_rows, value_rows, key_pos, log_all, delta_all, heads_count):

    def key_advance(carry, piece, start):
        query_part, attn_grad_part = piece
        count = query_part.shape[0]
        scores = jnp.einsum("qd,kd->qk", query_part, key_rows, preferred_element_type=jnp.float32)
        query_pos = jnp.arange(count, dtype=jnp.int32) // heads_count
        allowed = key_pos[None, :] <= query_pos[:, None]
        probs = jnp.where(
            allowed, jnp.exp(jnp.where(allowed, scores, -1e30) - log_all[:, None]), 0.0
        )
        grad_values = jnp.einsum(
            "qk,qd->kd",
            probs.astype(jnp.bfloat16),
            attn_grad_part,
            preferred_element_type=jnp.float32,
        )
        grad_probs = jnp.einsum(
            "qd,kd->qk", attn_grad_part, value_rows, preferred_element_type=jnp.float32
        )
        grad_scores = (probs * (grad_probs - delta_all[:, None])).astype(jnp.bfloat16)
        grad_keys = jnp.einsum(
            "qk,qd->kd", grad_scores, query_part, preferred_element_type=jnp.float32
        )
        return (grad_keys, grad_values)

    return key_advance


def local(hidden_in, norm_gain, qkv_weight, attn_cotangent):
    rows_in = hidden_in[0]
    grad_attn = attn_cotangent[0]
    tokens_here = rows_in.shape[0]
    width = rows_in.shape[1]
    head_size = HD
    heads_count = HEADS
    qcols = heads_count * head_size
    scale = head_size ** (-0.5)
    weight_group, gain_group = (
        lax.all_gather(qkv_weight, "intra", axis=0, tiled=True),
        lax.all_gather(norm_gain, "intra", axis=0, tiled=True),
    )
    weight_full, gain_full = (
        lax.all_gather(weight_group, "inter", axis=0, tiled=True),
        lax.all_gather(gain_group, "inter", axis=0, tiled=True),
    )
    query_pos = lax.axis_index("intra") * tokens_here + jnp.arange(tokens_here, dtype=jnp.int32)
    row_pos = jnp.broadcast_to(query_pos[:, None], (tokens_here, heads_count)).reshape(
        tokens_here * heads_count
    )
    cosine, sine = rope_tables(query_pos, head_size)
    wide_rows = rows_in.astype(jnp.float32)
    inv_rms = lax.rsqrt(jnp.mean(wide_rows * wide_rows, axis=1, keepdims=True) + eps_norm)
    normed = (wide_rows * inv_rms * gain_full.astype(jnp.float32)[None, :]).astype(jnp.bfloat16)
    mixed = jnp.dot(normed, weight_full, preferred_element_type=jnp.float32)
    query_rows = (
        (
            rotate(
                mixed[:, :qcols].reshape(tokens_here, heads_count, head_size),
                cosine[:, None, :],
                sine[:, None, :],
            )
            * scale
        )
        .astype(jnp.bfloat16)
        .reshape(tokens_here * heads_count, head_size)
    )
    key_rows = rotate(mixed[:, qcols : qcols + head_size], cosine, sine).astype(jnp.bfloat16)
    value_rows = mixed[:, qcols + head_size :].astype(jnp.bfloat16)
    grad_flat = grad_attn.reshape(tokens_here * heads_count, head_size)
    flat_rows = tokens_here * heads_count
    forward_step = forward_fold(query_rows, row_pos)
    start_carry = (
        jnp.full((flat_rows,), -1e30, jnp.float32),
        jnp.zeros((flat_rows,), jnp.float32),
        jnp.zeros((flat_rows, head_size), jnp.float32),
    )
    row_top, row_total, weighted = forward_step(
        start_carry,
        (
            lax.all_gather(key_rows, "intra", axis=0, tiled=True),
            lax.all_gather(value_rows, "intra", axis=0, tiled=True),
        ),
        jnp.int32(0),
    )
    attn_flat = (weighted / row_total[:, None]).astype(jnp.bfloat16)
    log_total = row_top + jnp.log(row_total)
    row_delta = jnp.sum(grad_flat.astype(jnp.float32) * attn_flat.astype(jnp.float32), axis=1)
    query_step = query_grad_fold(query_rows, row_pos, grad_flat, log_total, row_delta)
    grad_query = query_step(
        jnp.zeros((flat_rows, head_size), jnp.float32),
        (
            lax.all_gather(key_rows, "intra", axis=0, tiled=True),
            lax.all_gather(value_rows, "intra", axis=0, tiled=True),
        ),
        jnp.int32(0),
    )
    log_all, delta_all = (
        lax.all_gather(log_total, "intra", axis=0, tiled=True),
        lax.all_gather(row_delta, "intra", axis=0, tiled=True),
    )
    key_step = key_grad_fold(key_rows, value_rows, query_pos, log_all, delta_all, heads_count)
    grad_keys, grad_values = key_step(
        (
            jnp.zeros((tokens_here, head_size), jnp.float32),
            jnp.zeros((tokens_here, head_size), jnp.float32),
        ),
        (
            lax.all_gather(query_rows, "intra", axis=0, tiled=True),
            lax.all_gather(grad_flat, "intra", axis=0, tiled=True),
        ),
        jnp.int32(0),
    )
    query_back = (
        unrotate(
            grad_query.reshape(tokens_here, heads_count, head_size),
            cosine[:, None, :],
            sine[:, None, :],
        )
        * scale
    ).reshape(tokens_here, qcols)
    grad_mixed = jnp.concatenate(
        [query_back, unrotate(grad_keys, cosine, sine), grad_values], axis=1
    ).astype(jnp.bfloat16)
    weight_back, gain_back = (weight_full, gain_full)
    gain_wide = gain_back.astype(jnp.float32)[None, :]
    grad_normed = jnp.einsum(
        "tc,dc->td", grad_mixed, weight_back, preferred_element_type=jnp.float32
    )
    inner = jnp.sum(grad_normed * gain_wide * wide_rows, axis=1, keepdims=True)
    grad_rows = (
        gain_wide * grad_normed * inv_rms - wide_rows * inv_rms**3 / width * inner
    ).astype(jnp.bfloat16)
    gain_term = jnp.sum(grad_normed * wide_rows * inv_rms, axis=0)
    normed_cols = lax.all_to_all(normed, "intra", split_axis=1, concat_axis=0, tiled=True)
    group_term = lax.dot_general(
        normed_cols,
        lax.all_gather(grad_mixed, "intra", axis=0, tiled=True),
        (((0,), (0,)), ((), ())),
        preferred_element_type=jnp.float32,
    )
    term_low = lax.optimization_barrier(group_term.astype(jnp.bfloat16))
    gain_sums = lax.psum_scatter(gain_term, "intra", scatter_dimension=0, tiled=True)
    weight_grad, gain_grad = (
        lax.psum_scatter(term_low.astype(jnp.float32), "inter", scatter_dimension=0, tiled=True),
        lax.psum_scatter(gain_sums, "inter", scatter_dimension=0, tiled=True),
    )
    return (attn_flat.reshape(tokens_here, qcols)[None], grad_rows[None], weight_grad, gain_grad)

MESH = pl.DeviceIdType.MESH
CORES = 2
SIDE = 2
GAIN_ROWS = 16


def nt_dot(a, b):
    return lax.dot_general(a, b, (((1,), (1,)), ((), ())), preferred_element_type=jnp.float32)


def tn_dot(a, b):
    return lax.dot_general(a, b, (((0,), (0,)), ((), ())), preferred_element_type=jnp.float32)


def nn_dot(a, b):
    return jnp.dot(a, b, preferred_element_type=jnp.float32)


def fused_kernel(
    n_inter,
    hid_ref, gain_ref, w_ref, ct_ref, cos_ref, sin_ref,
    attn_ref, gin_ref, wg_ref, gg_ref,
    wbuf, nrm, nbuf, kvbuf, gkv, gkv_out, gkv_in, gmbuf, tbuf, rs1, ybuf, rs2, zbuf, rs3, mix,
    ag_send, ag_recv, ex_send, ex_recv, c_send, c_recv, y_send, y_recv, z_send, z_recv,
):
    i = lax.axis_index("inter")
    x = lax.axis_index("intra")
    nz = n_inter // (CORES * SIDE)
    c = lax.rem(i, CORES)
    y = lax.rem(i // CORES, SIDE)
    z = i // (CORES * SIDE)
    toks, width = hid_ref.shape
    rows, cols = w_ref.shape
    half = width // 2
    qcols = HEADS * HD
    scale = HD ** (-0.5)

    def dev(zz, yy, cc, xx):
        return ((zz * SIDE + yy) * CORES + cc, xx)

    def slot(zz, yy, cc, xx):
        return ((zz * SIDE + yy) * CORES + cc) * 2 + xx

    x_peer = dev(z, y, c, 1 - x)
    y_peer = dev(z, 1 - y, c, x)
    c_peer = dev(z, y, 1 - c, x)

    def z_peer(zz):
        return dev(zz, y, c, x)

    own = slot(z, y, c, x)
    wbuf[own, :rows, :] = w_ref[...]
    wbuf[own, rows:, :HD] = jnp.broadcast_to(gain_ref[...], (GAIN_ROWS, HD))
    wbuf[own, rows:, HD:] = jnp.zeros((GAIN_ROWS, cols - HD), jnp.bfloat16)

    barrier = pltpu.get_barrier_semaphore()
    peers = [x_peer, y_peer, c_peer] + [z_peer(lax.rem(z + d, nz)) for d in range(1, nz)]
    for peer in peers:
        pl.semaphore_signal(barrier, inc=1, device_id=peer, device_id_type=MESH)
    pl.semaphore_wait(barrier, len(peers))

    targets = {
        0: x_peer,
        1: y_peer,
        2: z_peer(jnp.minimum(z + 1, nz - 1)),
        3: z_peer(jnp.maximum(z - 1, 0)),
        4: c_peer,
    }
    sent = []

    def ag(link, g):
        return pltpu.make_async_remote_copy(
            src_ref=wbuf.at[g], dst_ref=wbuf.at[g],
            send_sem=ag_send.at[link, g], recv_sem=ag_recv.at[g],
            device_id=targets[link], device_id_type=MESH,
        )

    def send(link, g, cond=None):
        sent.append((link, g, cond))
        if cond is None:
            ag(link, g).start()
        else:
            pl.when(cond)(lambda: ag(link, g).start())

    def arrive(g, cond=None):
        if cond is None:
            ag(0, g).wait_recv()
        else:
            pl.when(cond)(lambda: ag(0, g).wait_recv())

    def both(a, b):
        return b if a is None else jnp.logical_and(a, b)

    up, down = z < nz - 1, z > 0
    send(0, own)
    send(1, own)
    send(2, own, up)
    send(3, own, down)
    send(4, own)
    wide = hid_ref[...].astype(jnp.float32)
    inv = lax.rsqrt(jnp.mean(wide * wide, axis=1, keepdims=True) + eps_norm)
    mix[...] = jnp.zeros((toks, cols), jnp.float32)
    span = lambda g: pl.ds(pl.multiple_of(g * rows, rows), rows)

    def absorb(g):
        gain = wbuf[g, rows : rows + 1, :rows].astype(jnp.float32)
        part = (hid_ref[:, span(g)].astype(jnp.float32) * inv * gain).astype(jnp.bfloat16)
        nrm[:, span(g)] = part
        mix[...] += nn_dot(part, wbuf[g, :rows, :])

    def absorb_when(g, cond):
        if cond is None:
            absorb(g)
        else:
            pl.when(cond)(lambda: absorb(g))

    def sides(d):
        if d == 0:
            return [(z, None, None)]
        return [(z - d, z - d >= 0, 2), (z + d, z + d < nz, 3)]

    def onward(link):
        return up if link == 2 else down

    late = []

    def done(zz, yy, xx, ok):
        late.append((zz, yy, xx, ok))
        absorb_when(slot(zz, yy, c, xx), ok)

    def drain(count):
        for _ in range(min(count, len(late))):
            zz, yy, xx, ok = late.pop(0)
            g = slot(zz, yy, 1 - c, xx)
            arrive(g, ok)
            absorb_when(g, ok)

    def column(d):
        for zz, ok, link in sides(d):
            g = slot(zz, y, c, x)
            arrive(g, ok)
            send(link, g, both(ok, onward(link)))
            for k in (0, 1, 4):
                send(k, g, ok)
        for zz, ok, link in sides(d):
            done(zz, y, x, ok)

    direct = [d for d in range(nz) if d == 0 or d >= 3]

    def side(d):
        for zz, ok, link in sides(d):
            odd = lax.rem(zz + 2 * nz, 2) == 1
            g = slot(zz, y, c, 1 - x)
            arrive(g, ok)
            if d in direct:
                send(1, g, both(ok, odd))
            send(4, g, ok)
            g = slot(zz, 1 - y, c, x)
            arrive(g, ok)
            if d in direct:
                send(0, g, both(ok, jnp.logical_not(odd)))
            send(4, g, ok)
        for zz, ok, link in sides(d):
            done(zz, y, 1 - x, ok)
            done(zz, 1 - y, x, ok)

    def diagonal(d):
        for zz, ok, link in sides(d):
            g = slot(zz, 1 - y, c, 1 - x)
            arrive(g, ok)
            if d + 1 < nz and d + 1 not in direct:
                if d == 0:
                    send(2, g, up)
                    send(3, g, down)
                else:
                    send(link, g, both(ok, onward(link)))
            send(4, g, ok)
        for zz, ok, link in sides(d):
            done(zz, 1 - y, 1 - x, ok)

    done(z, y, x, None)
    steps = [(d * 3, column, d) for d in range(1, nz)]
    steps += [(d * 3 + 4, side, d) for d in range(nz)]
    steps += [(d * 3 + 8, diagonal, d) for d in range(nz)]
    for _, step, d in sorted(steps, key=lambda e: e[0]):
        waiting = len(late)
        step(d)
        drain(waiting)
    drain(len(late))
    acc = mix[...]

    cosine = cos_ref[pl.ds(pl.multiple_of(x * toks, toks), toks), :]
    sine = sin_ref[pl.ds(pl.multiple_of(x * toks, toks), toks), :]

    def rope(u):
        return u * cosine + pltpu.roll(u, HD // 2, 1) * sine

    def unrope(u):
        return u * cosine - pltpu.roll(u, HD // 2, 1) * sine

    here = pl.ds(pl.multiple_of(x * toks, toks), toks)
    there = pl.ds(pl.multiple_of((1 - x) * toks, toks), toks)

    def exchange(k, src, dst):
        return pltpu.make_async_remote_copy(
            src_ref=src, dst_ref=dst, send_sem=ex_send.at[k], recv_sem=ex_recv.at[k],
            device_id=x_peer, device_id_type=MESH,
        )

    kvbuf[here, :HD] = rope(acc[:, qcols : qcols + HD]).astype(jnp.bfloat16)
    kvbuf[here, HD:] = acc[:, qcols + HD :].astype(jnp.bfloat16)
    query = [(rope(acc[:, h * HD : (h + 1) * HD]) * scale).astype(jnp.bfloat16) for h in range(HEADS)]
    query = jnp.concatenate(query, axis=0)
    kv_copy = exchange(0, kvbuf.at[here], kvbuf.at[here])
    kv_copy.start()
    keep = pl.ds(pl.multiple_of(x * half, half), half)
    part = half // 2
    norm_copy, norm_rest = [
        exchange(
            k,
            nrm.at[:, pl.ds(pl.multiple_of((1 - x) * half + first, part), part)],
            nbuf.at[here, first : first + part],
        )
        for k, first in ((1, 0), (4, part))
    ]
    norm_copy.start()
    nbuf[here, :] = nrm[:, keep]
    kv_copy.wait()

    flat = HEADS * toks
    keys, values = kvbuf[:, :HD], kvbuf[:, HD:]
    row_pos = x * toks + lax.rem(lax.broadcasted_iota(jnp.int32, (flat, 2 * toks), 0), toks)
    allowed = lax.broadcasted_iota(jnp.int32, (flat, 2 * toks), 1) <= row_pos
    scores = jnp.where(allowed, nt_dot(query, keys), -1e30)
    top = jnp.max(scores, axis=1, keepdims=True)
    numbers = jnp.where(allowed, jnp.exp(scores - top), 0.0)
    total = jnp.sum(numbers, axis=1, keepdims=True)
    high = numbers.astype(jnp.bfloat16)
    low = (numbers - high.astype(jnp.float32)).astype(jnp.bfloat16)
    attn = ((nn_dot(high, values) + nn_dot(low, values)) / total).astype(jnp.bfloat16)
    for h in range(HEADS):
        attn_ref[:, h * HD : (h + 1) * HD] = attn[h * toks : (h + 1) * toks]
    grad = jnp.concatenate([ct_ref[:, h * HD : (h + 1) * HD] for h in range(HEADS)], axis=0)
    delta = jnp.sum(grad.astype(jnp.float32) * attn.astype(jnp.float32), axis=1, keepdims=True)
    probs = numbers / total
    grad_scores = (probs * (nt_dot(grad, values) - delta)).astype(jnp.bfloat16)
    gkv[:, :HD] = tn_dot(grad_scores, query)
    gkv[:, HD:] = tn_dot(probs.astype(jnp.bfloat16), grad)
    gkv_out[...] = gkv[there, :].astype(jnp.bfloat16)
    gkv_copy = exchange(2, gkv_out, gkv_in)
    gkv_copy.start()
    norm_rest.start()
    grad_query = nn_dot(grad_scores, keys)
    for h in range(HEADS):
        gmbuf[here, h * HD : (h + 1) * HD] = (
            unrope(grad_query[h * toks : (h + 1) * toks]) * scale
        ).astype(jnp.bfloat16)
    gkv_copy.wait()
    own_kv = gkv[here, :] + gkv_in[...].astype(jnp.float32)
    gmbuf[here, qcols : qcols + HD] = unrope(own_kv[:, :HD]).astype(jnp.bfloat16)
    gmbuf[here, qcols + HD :] = own_kv[:, HD:].astype(jnp.bfloat16)
    gm_copy = exchange(3, gmbuf.at[here], gmbuf.at[here])
    gm_copy.start()

    gm = gmbuf[here, :]
    inner = jnp.sum(gm.astype(jnp.float32) * mix[...], axis=1, keepdims=True)
    back = inner * (inv * inv / width)

    def grad_rows(first, last):
        for g in range(first, last):
            lanes = slice(g * rows, (g + 1) * rows)
            gain = wbuf[g, rows : rows + 1, :rows].astype(jnp.float32)
            part = nt_dot(gm, wbuf[g, :rows, :])
            gin_ref[:, lanes] = (
                gain * part * inv - hid_ref[:, lanes].astype(jnp.float32) * back
            ).astype(jnp.bfloat16)

    pieces = nz + 1
    marks = [2 * n_inter * k // pieces for k in range(pieces + 1)]
    grad_rows(marks[0], marks[1])
    norm_copy.wait()
    norm_rest.wait()
    gm_copy.wait()

    both_gm = gmbuf[...]

    def term(k, cc):
        j = k * CORES + cc
        lanes = pl.ds(pl.multiple_of(j * rows, rows), rows)
        tbuf[j] = tn_dot(nbuf[:, lanes], both_gm).astype(jnp.bfloat16)

    def to_core(k):
        return pltpu.make_async_remote_copy(
            src_ref=tbuf.at[k * CORES + 1 - c], dst_ref=rs1.at[k],
            send_sem=c_send.at[k], recv_sem=c_recv.at[k], device_id=c_peer, device_id_type=MESH,
        )

    def to_y(zz):
        return pltpu.make_async_remote_copy(
            src_ref=ybuf.at[zz], dst_ref=rs2.at[zz],
            send_sem=y_send.at[zz], recv_sem=y_recv.at[zz], device_id=y_peer, device_id_type=MESH,
        )

    def to_z(d):
        return pltpu.make_async_remote_copy(
            src_ref=zbuf.at[d - 1], dst_ref=rs3.at[d - 1],
            send_sem=z_send.at[d - 1], recv_sem=z_recv.at[d - 1],
            device_id=z_peer(lax.rem(z + d, nz)), device_id_type=MESH,
        )

    order = [(d, lax.rem(z + d, nz)) for d in list(range(1, nz)) + [0]]

    def core_sum(k):
        to_core(k).wait_recv()
        return tbuf[k * CORES + c].astype(jnp.float32) + rs1[k].astype(jnp.float32)

    def to_y_side(zz):
        ybuf[zz] = core_sum(zz * SIDE + 1 - y).astype(jnp.bfloat16)
        to_y(zz).start()

    last = None
    for d, zz in order:
        k = zz * SIDE + 1 - y
        term(k, 1 - c)
        to_core(k).start()
        term(k, c)
        if last is not None:
            to_y_side(last)
        last = zz
    for n, (d, zz) in enumerate(order):
        k = zz * SIDE + y
        term(k, 1 - c)
        to_core(k).start()
        if n == 0:
            to_y_side(last)
        term(k, c)
    for n, (d, zz) in enumerate(order):
        grad_rows(marks[n + 1], marks[n + 2])
        part = core_sum(zz * SIDE + y)
        to_y(zz).wait_recv()
        part = part + rs2[zz].astype(jnp.float32)
        if d:
            zbuf[d - 1] = part.astype(jnp.bfloat16)
            to_z(d).start()
        else:
            wg_ref[...] = part
    result = wg_ref[...]
    for d in range(1, nz):
        to_z(d).wait_recv()
        result = result + rs3[d - 1].astype(jnp.float32)
    wg_ref[...] = result
    block = x * n_inter + i
    mixed_sum = wbuf[block, :rows, :].astype(jnp.float32) * result
    lanes_sum = mixed_sum[:, :HD]
    for k in range(1, cols // HD):
        lanes_sum = lanes_sum + mixed_sum[:, k * HD : (k + 1) * HD]
    gain = wbuf[block, rows : rows + 1, :rows].astype(jnp.float32)
    gg_ref[...] = jnp.sum(lanes_sum.T, axis=0, keepdims=True) / gain

    for link, g, cond in sent:
        if cond is None:
            ag(link, g).wait_send()
        else:
            pl.when(cond)(functools.partial(lambda l, s: ag(l, s).wait_send(), link, g))
    for k in range(nz * SIDE):
        to_core(k).wait_send()
    for zz in range(nz):
        to_y(zz).wait_send()
    for d in range(1, nz):
        to_z(d).wait_send()


def copy_kernel(*refs):
    for k in range(4):
        refs[4 + k][...] = refs[k][...]


def fused(n_inter, hidden_in, norm_gain, qkv_weight, attn_cotangent):
    toks, width = hidden_in.shape[1:]
    rows, cols = qkv_weight.shape
    nz = n_inter // (CORES * SIDE)
    chips = nz * SIDE
    freqs = rope_base ** (-np.arange(HD // 2, dtype=np.float32) / np.float32(HD // 2))
    angles = (np.arange(2 * toks, dtype=np.float32)[:, None] * freqs.astype(np.float32)[None, :]).astype(np.float32)
    cosine = np.concatenate([np.cos(angles)] * 2, axis=1).astype(np.float32)
    sine = np.concatenate([-np.sin(angles), np.sin(angles)], axis=1).astype(np.float32)
    bf, f32, dma = jnp.bfloat16, jnp.float32, pltpu.SemaphoreType.DMA
    vmem = pl.BlockSpec(memory_space=pltpu.VMEM)
    attn, gin, wg, gg = pl.pallas_call(
        functools.partial(fused_kernel, n_inter),
        out_shape=(
            jax.ShapeDtypeStruct((toks, HEADS * HD), bf),
            jax.ShapeDtypeStruct((toks, width), bf),
            jax.ShapeDtypeStruct((rows, cols), f32),
            jax.ShapeDtypeStruct((1, rows), f32),
        ),
        in_specs=[vmem] * 6,
        out_specs=(vmem,) * 4,
        scratch_shapes=[
            pltpu.VMEM((2 * n_inter, rows + GAIN_ROWS, cols), bf),
            pltpu.VMEM((toks, width), bf),
            pltpu.VMEM((2 * toks, width // 2), bf),
            pltpu.VMEM((2 * toks, 2 * HD), bf),
            pltpu.VMEM((2 * toks, 2 * HD), f32),
            pltpu.VMEM((toks, 2 * HD), bf),
            pltpu.VMEM((toks, 2 * HD), bf),
            pltpu.VMEM((2 * toks, cols), bf),
            pltpu.VMEM((n_inter, rows, cols), bf),
            pltpu.VMEM((chips, rows, cols), bf),
            pltpu.VMEM((nz, rows, cols), bf),
            pltpu.VMEM((nz, rows, cols), bf),
            pltpu.VMEM((max(nz - 1, 1), rows, cols), bf),
            pltpu.VMEM((max(nz - 1, 1), rows, cols), bf),
            pltpu.VMEM((toks, cols), f32),
            dma((5, 2 * n_inter)), dma((2 * n_inter,)),
            dma((5,)), dma((5,)),
            dma((chips,)), dma((chips,)),
            dma((nz,)), dma((nz,)),
            dma((max(nz - 1, 1),)), dma((max(nz - 1, 1),)),
        ],
        compiler_params=pltpu.CompilerParams(
            collective_id=0, has_side_effects=True, vmem_limit_bytes=60 * 2**20
        ),
    )(hidden_in[0], norm_gain[None], qkv_weight, attn_cotangent[0], cosine, sine)
    outs = (attn, gin, wg, gg)
    attn, gin, wg, gg = pl.pallas_call(
        copy_kernel,
        out_shape=tuple(jax.ShapeDtypeStruct(o.shape, o.dtype) for o in outs),
        in_specs=[vmem] * 4,
        out_specs=(vmem,) * 4,
    )(*outs)
    return attn[None], gin[None], wg, gg[0]


def solution(mesh):
    n_inter, n_intra = mesh.shape["inter"], mesh.shape["intra"]

    def body(hidden_in, norm_gain, qkv_weight, attn_cotangent):
        fits = n_intra == 2 and n_inter % (CORES * SIDE) == 0
        fits = fits and qkv_weight.shape[0] == HD and hidden_in.shape[0] == 1
        fits = fits and hidden_in.shape[1] % HD == 0
        if fits:
            return fused(n_inter, hidden_in, norm_gain, qkv_weight, attn_cotangent)
        return local(hidden_in, norm_gain, qkv_weight, attn_cotangent)

    return jax.shard_map(
        body,
        mesh=mesh,
        in_specs=(
            P("inter", "intra", None),
            P(("inter", "intra")),
            P(("inter", "intra"), None),
            P("inter", "intra", None),
        ),
        out_specs=(
            P("inter", "intra", None),
            P("inter", "intra", None),
            P(("intra", "inter"), None),
            P(("intra", "inter")),
        ),
        check_vma=False,
    )
```

profile of v0, /device:TPU:0, one launch (start us, length us, event | category | flops | bytes accessed | tf_op | source)
XLA Modules:
  0.0 94.8 jit_solution(10986652774129804330)
XLA Ops:
  0.6 91.6 %shard_map.93 = (bf16[128,512]{1,0:T(8,128)(2,1)}, bf16[128,4096]{1,0:T(8,128)(2,1)}, f32[128,768]{1,0:T(8,128)}, f32[1,128]{1,0:T(1,128)}) custom-call(bf16[128,4096]{1,0:T(8,128)(2,1)} %bitcast.6, bf16[1,128]{1,0:T(2,128)(2,1)} %bitcast.8, bf16[128,768]{1,0:T(8,128)(2,1)} %w_ref.1, bf16[128,512]{1,0:T(8,128)(2,1)} %bitcast.7, ...), custom_call_target="tpu_custom_call" | custom-call | tf_op jit(solution)/shard_map/pallas_call | solution.py:620
  92.2 2.6 %shard_map.94 = (bf16[128,512]{1,0:T(8,128)(2,1)}, bf16[128,4096]{1,0:T(8,128)(2,1)}, f32[128,768]{1,0:T(8,128)}, f32[1,128]{1,0:T(1,128)}) custom-call(bf16[128,512]{1,0:T(8,128)(2,1)} %get-tuple-element.12.refs_0_, bf16[128,4096]{1,0:T(8,128)(2,1)} %get-tuple-element.13.refs_1_, f32[128,768]{1,0:T(8,128)} %get-tuple-element.14.refs_2_, ...), custom_call_target="tpu_custom_call" | custom-call | tf_op jit(solution)/shard_map/pallas_call | solution.py:657
where the time goes:
time: 95 us; the launch traced here: 94.8 us
  Pallas kernels  94.2 us (99%)
    pallas_call x1, Pallas kernels, fused(): pl.pallas_call(functools.partial(fused_kernel, n_inter), out_shape=(jax.S...  91.6 us
    pallas_call x1, Pallas kernels, fused(): pl.pallas_call(copy_kernel, out_shape=tuple((jax.ShapeDtypeStruct(o.shape...  2.56 us

commit v1 on v0

v1 whole, which is shorter than its diff:
```python
import functools
import jax
import jax.numpy as jnp
import numpy as np
from jax import lax
from jax.experimental import pallas as pl
from jax.experimental.pallas import tpu as pltpu
from jax.sharding import PartitionSpec as P

HD = 128
HEADS = 4


eps_norm = 1e-05
rope_base = 500000.0


def rope_tables(positions, head_size):
    half_size = head_size // 2
    freqs = rope_base ** (-jnp.arange(half_size, dtype=jnp.float32) / half_size)
    angles = positions.astype(jnp.float32)[:, None] * freqs[None, :]
    return (jnp.cos(angles), jnp.sin(angles))


def rotate(values_in, cosine, sine):
    half_size = values_in.shape[-1] // 2
    first, second = (values_in[..., :half_size], values_in[..., half_size:])
    return jnp.concatenate(
        [first * cosine - second * sine, second * cosine + first * sine], axis=-1
    )


def unrotate(grad_out, cosine, sine):
    half_size = grad_out.shape[-1] // 2
    first, second = (grad_out[..., :half_size], grad_out[..., half_size:])
    return jnp.concatenate(
        [first * cosine + second * sine, second * cosine - first * sine], axis=-1
    )


def forward_fold(query_rows, row_pos):

    def forward_advance(carry, piece, start):
        row_top, row_total, weighted = carry
        key_part, value_part = piece
        scores = jnp.einsum("qd,kd->qk", query_rows, key_part, preferred_element_type=jnp.float32)
        key_pos = jnp.arange(key_part.shape[0], dtype=jnp.int32)
        allowed = key_pos[None, :] <= row_pos[:, None]
        scores = jnp.where(allowed, scores, -1e30)
        new_top = jnp.maximum(row_top, jnp.max(scores, axis=1))
        numbers = jnp.where(allowed, jnp.exp(scores - new_top[:, None]), 0.0)
        row_total = jnp.sum(numbers, axis=1)
        weighted = jnp.dot(
            numbers,
            value_part.astype(jnp.float32),
            precision=lax.Precision.HIGHEST,
            preferred_element_type=jnp.float32,
        )
        return (new_top, row_total, weighted)

    return forward_advance


def query_grad_fold(query_rows, row_pos, grad_flat, log_total, row_delta):

    def query_advance(grad_query, piece, start):
        key_part, value_part = piece
        scores = jnp.einsum("qd,kd->qk", query_rows, key_part, preferred_element_type=jnp.float32)
        key_pos = jnp.arange(key_part.shape[0], dtype=jnp.int32)
        allowed = key_pos[None, :] <= row_pos[:, None]
        probs = jnp.where(
            allowed, jnp.exp(jnp.where(allowed, scores, -1e30) - log_total[:, None]), 0.0
        )
        grad_probs = jnp.einsum(
            "qd,kd->qk", grad_flat, value_part, preferred_element_type=jnp.float32
        )
        grad_scores = (probs * (grad_probs - row_delta[:, None])).astype(jnp.bfloat16)
        return jnp.dot(grad_scores, key_part, preferred_element_type=jnp.float32)

    return query_advance


def key_grad_fold(key_rows, value_rows, key_pos, log_all, delta_all, heads_count):

    def key_advance(carry, piece, start):
        query_part, attn_grad_part = piece
        count = query_part.shape[0]
        scores = jnp.einsum("qd,kd->qk", query_part, key_rows, preferred_element_type=jnp.float32)
        query_pos = jnp.arange(count, dtype=jnp.int32) // heads_count
        allowed = key_pos[None, :] <= query_pos[:, None]
        probs = jnp.where(
            allowed, jnp.exp(jnp.where(allowed, scores, -1e30) - log_all[:, None]), 0.0
        )
        grad_values = jnp.einsum(
            "qk,qd->kd",
            probs.astype(jnp.bfloat16),
            attn_grad_part,
            preferred_element_type=jnp.float32,
        )
        grad_probs = jnp.einsum(
            "qd,kd->qk", attn_grad_part, value_rows, preferred_element_type=jnp.float32
        )
        grad_scores = (probs * (grad_probs - delta_all[:, None])).astype(jnp.bfloat16)
        grad_keys = jnp.einsum(
            "qk,qd->kd", grad_scores, query_part, preferred_element_type=jnp.float32
        )
        return (grad_keys, grad_values)

    return key_advance


def local(hidden_in, norm_gain, qkv_weight, attn_cotangent):
    rows_in = hidden_in[0]
    grad_attn = attn_cotangent[0]
    tokens_here = rows_in.shape[0]
    width = rows_in.shape[1]
    head_size = HD
    heads_count = HEADS
    qcols = heads_count * head_size
    scale = head_size ** (-0.5)
    weight_group, gain_group = (
        lax.all_gather(qkv_weight, "intra", axis=0, tiled=True),
        lax.all_gather(norm_gain, "intra", axis=0, tiled=True),
    )
    weight_full, gain_full = (
        lax.all_gather(weight_group, "inter", axis=0, tiled=True),
        lax.all_gather(gain_group, "inter", axis=0, tiled=True),
    )
    query_pos = lax.axis_index("intra") * tokens_here + jnp.arange(tokens_here, dtype=jnp.int32)
    row_pos = jnp.broadcast_to(query_pos[:, None], (tokens_here, heads_count)).reshape(
        tokens_here * heads_count
    )
    cosine, sine = rope_tables(query_pos, head_size)
    wide_rows = rows_in.astype(jnp.float32)
    inv_rms = lax.rsqrt(jnp.mean(wide_rows * wide_rows, axis=1, keepdims=True) + eps_norm)
    normed = (wide_rows * inv_rms * gain_full.astype(jnp.float32)[None, :]).astype(jnp.bfloat16)
    mixed = jnp.dot(normed, weight_full, preferred_element_type=jnp.float32)
    query_rows = (
        (
            rotate(
                mixed[:, :qcols].reshape(tokens_here, heads_count, head_size),
                cosine[:, None, :],
                sine[:, None, :],
            )
            * scale
        )
        .astype(jnp.bfloat16)
        .reshape(tokens_here * heads_count, head_size)
    )
    key_rows = rotate(mixed[:, qcols : qcols + head_size], cosine, sine).astype(jnp.bfloat16)
    value_rows = mixed[:, qcols + head_size :].astype(jnp.bfloat16)
    grad_flat = grad_attn.reshape(tokens_here * heads_count, head_size)
    flat_rows = tokens_here * heads_count
    forward_step = forward_fold(query_rows, row_pos)
    start_carry = (
        jnp.full((flat_rows,), -1e30, jnp.float32),
        jnp.zeros((flat_rows,), jnp.float32),
        jnp.zeros((flat_rows, head_size), jnp.float32),
    )
    row_top, row_total, weighted = forward_step(
        start_carry,
        (
            lax.all_gather(key_rows, "intra", axis=0, tiled=True),
            lax.all_gather(value_rows, "intra", axis=0, tiled=True),
        ),
        jnp.int32(0),
    )
    attn_flat = (weighted / row_total[:, None]).astype(jnp.bfloat16)
    log_total = row_top + jnp.log(row_total)
    row_delta = jnp.sum(grad_flat.astype(jnp.float32) * attn_flat.astype(jnp.float32), axis=1)
    query_step = query_grad_fold(query_rows, row_pos, grad_flat, log_total, row_delta)
    grad_query = query_step(
        jnp.zeros((flat_rows, head_size), jnp.float32),
        (
            lax.all_gather(key_rows, "intra", axis=0, tiled=True),
            lax.all_gather(value_rows, "intra", axis=0, tiled=True),
        ),
        jnp.int32(0),
    )
    log_all, delta_all = (
        lax.all_gather(log_total, "intra", axis=0, tiled=True),
        lax.all_gather(row_delta, "intra", axis=0, tiled=True),
    )
    key_step = key_grad_fold(key_rows, value_rows, query_pos, log_all, delta_all, heads_count)
    grad_keys, grad_values = key_step(
        (
            jnp.zeros((tokens_here, head_size), jnp.float32),
            jnp.zeros((tokens_here, head_size), jnp.float32),
        ),
        (
            lax.all_gather(query_rows, "intra", axis=0, tiled=True),
            lax.all_gather(grad_flat, "intra", axis=0, tiled=True),
        ),
        jnp.int32(0),
    )
    query_back = (
        unrotate(
            grad_query.reshape(tokens_here, heads_count, head_size),
            cosine[:, None, :],
            sine[:, None, :],
        )
        * scale
    ).reshape(tokens_here, qcols)
    grad_mixed = jnp.concatenate(
        [query_back, unrotate(grad_keys, cosine, sine), grad_values], axis=1
    ).astype(jnp.bfloat16)
    weight_back, gain_back = (weight_full, gain_full)
    gain_wide = gain_back.astype(jnp.float32)[None, :]
    grad_normed = jnp.einsum(
        "tc,dc->td", grad_mixed, weight_back, preferred_element_type=jnp.float32
    )
    inner = jnp.sum(grad_normed * gain_wide * wide_rows, axis=1, keepdims=True)
    grad_rows = (
        gain_wide * grad_normed * inv_rms - wide_rows * inv_rms**3 / width * inner
    ).astype(jnp.bfloat16)
    gain_term = jnp.sum(grad_normed * wide_rows * inv_rms, axis=0)
    normed_cols = lax.all_to_all(normed, "intra", split_axis=1, concat_axis=0, tiled=True)
    group_term = lax.dot_general(
        normed_cols,
        lax.all_gather(grad_mixed, "intra", axis=0, tiled=True),
        (((0,), (0,)), ((), ())),
        preferred_element_type=jnp.float32,
    )
    term_low = lax.optimization_barrier(group_term.astype(jnp.bfloat16))
    gain_sums = lax.psum_scatter(gain_term, "intra", scatter_dimension=0, tiled=True)
    weight_grad, gain_grad = (
        lax.psum_scatter(term_low.astype(jnp.float32), "inter", scatter_dimension=0, tiled=True),
        lax.psum_scatter(gain_sums, "inter", scatter_dimension=0, tiled=True),
    )
    return (attn_flat.reshape(tokens_here, qcols)[None], grad_rows[None], weight_grad, gain_grad)

MESH = pl.DeviceIdType.MESH
CORES = 2
SIDE = 2
PIECES = 4
CHUNK = 2 * HD


def nt_dot(a, b):
    return lax.dot_general(a, b, (((1,), (1,)), ((), ())), preferred_element_type=jnp.float32)


def tn_dot(a, b):
    return lax.dot_general(a, b, (((0,), (0,)), ((), ())), preferred_element_type=jnp.float32)


def nn_dot(a, b):
    return jnp.dot(a, b, preferred_element_type=jnp.float32)


def fused_kernel(
    n_inter,
    hid_ref, gain_ref, w_ref, ct_ref, cos_hbm, sin_hbm,
    attn_ref, gin_ref, wg_ref, gg_ref,
    wbuf, gbuf, gain_in, hx, hs, nbuf, ntr, inv_all, inv_s, inv_r, ctb, cts, cos_ref, sin_ref,
    mix, kv_s, kv_r, qm_s, qm_r, gq, gkv_s, gkv_r, gkv, in_s, in_r, at_s, at_r, gi_s, gi_r,
    tbuf, rs1, ybuf, rs2, zbuf, rs3, dg_s, dg_r, gg_s, gg_r,
    ld_sem, ag_send, ag_recv, g_send, g_recv, x_send, x_recv,
    c_send, c_recv, y_send, y_recv, z_send, z_recv, d_send, d_recv,
):
    i = lax.axis_index("inter")
    x = lax.axis_index("intra")
    nz = n_inter // (CORES * SIDE)
    c = lax.rem(i, CORES)
    y = lax.rem(i // CORES, SIDE)
    z = i // (CORES * SIDE)
    toks, width = hid_ref.shape
    rows, cols = w_ref.shape
    seq = 2 * toks
    qcols = HEADS * HD
    chips = nz * SIDE
    chunks = cols // CHUNK
    span = n_inter // PIECES
    lanes = span * rows
    scale = HD ** (-0.5)
    f32, bf = jnp.float32, jnp.bfloat16

    def dev(zz, yy, cc, xx):
        return ((zz * SIDE + yy) * CORES + cc, xx)

    def slot(zz, yy, cc):
        return (zz * SIDE + yy) * CORES + cc

    def across(d):
        zz, bit = z, 1
        while bit < nz:
            if d & bit:
                zz = zz + bit - 2 * bit * lax.rem(z // bit, 2)
            bit *= 2
        return zz

    hops = list(range(1, nz))
    x_peer = dev(z, y, c, 1 - x)
    y_peer = dev(z, 1 - y, c, x)
    c_peer = dev(z, y, 1 - c, x)
    d_peer = dev(z, y, 1 - c, 1 - x)
    plane = [(d, yy, cc) for d in range(nz) for yy in (0, 1) for cc in (0, 1) if d or yy or cc]

    def plane_dev(e):
        d, yy, cc = e
        return (across(d), y + yy - 2 * yy * y, c + cc - 2 * cc * c)

    own = slot(z, y, c)
    here = pl.ds(pl.multiple_of(x * toks, toks), toks)
    there = pl.ds(pl.multiple_of((1 - x) * toks, toks), toks)

    def rcopy(src, dst, ss, rs, device):
        return pltpu.make_async_remote_copy(
            src_ref=src, dst_ref=dst, send_sem=ss, recv_sem=rs, device_id=device, device_id_type=MESH
        )

    barrier = pltpu.get_barrier_semaphore()
    peers = [dev(*plane_dev(e), x) for e in plane] + [x_peer, d_peer]
    for peer in peers:
        pl.semaphore_signal(barrier, inc=1, device_id=peer, device_id_type=MESH)

    def load(src, dst, k):
        pltpu.make_async_copy(src, dst, ld_sem.at[k]).start()

    def loaded(dst, k):
        pltpu.make_async_copy(dst, dst, ld_sem.at[k]).wait()

    for p in range(PIECES):
        for b in range(span):
            j = p * span + b
            mine = pl.ds(pl.multiple_of((2 * j + x) * rows, rows), rows)
            other = pl.ds(pl.multiple_of((2 * j + 1 - x) * rows, rows), rows)
            load(hid_ref.at[:, mine], hx.at[p, here, b * rows : (b + 1) * rows], 0)
            load(hid_ref.at[:, other], hs.at[p, :, b * rows : (b + 1) * rows], 1)
    load(w_ref.at[:, qcols:], wbuf.at[0, own], 2)
    half = HEADS // 2
    for n in range(half):
        for xx in range(2):
            first = (xx * half + n) * HD
            load(w_ref.at[:, first : first + HD], wbuf.at[1 + n, own, :, xx * HD : (xx + 1) * HD], 3 + n)
    nxt = 3 + half
    load(gain_ref, gain_in, nxt)
    load(ct_ref.at[:, pl.ds(pl.multiple_of(x * half * HD, HD), half * HD)], ctb.at[here], nxt + 1)
    load(ct_ref.at[:, pl.ds(pl.multiple_of((1 - x) * half * HD, HD), half * HD)], cts, nxt + 2)
    load(cos_hbm, cos_ref, nxt + 3)
    load(sin_hbm, sin_ref, nxt + 4)

    loaded(gain_in, nxt)
    gcol = lambda g: pl.ds(pl.multiple_of(g * rows, rows), rows)
    gbuf[:, gcol(own)] = gain_in[...].astype(f32)
    loaded(hx.at[:, here], 0)
    loaded(hs, 1)
    total = jnp.zeros((toks, 1), f32)
    for p in range(PIECES):
        a = hx[p, here, :].astype(f32)
        b = hs[p].astype(f32)
        total = total + jnp.sum(a * a + b * b, axis=1, keepdims=True)
    inv = jnp.broadcast_to(lax.rsqrt(total / width + eps_norm), (toks, HD))
    inv_all[here, :] = inv
    inv_s[...] = inv.T[:8, :]
    for q in range(chunks):
        loaded(wbuf.at[q, own], 2 + q)
    loaded(cts, nxt + 2)
    pl.semaphore_wait(barrier, len(peers))

    def ag(q, g, link, device):
        return rcopy(wbuf.at[q, g], wbuf.at[q, g], ag_send.at[q, link], ag_recv.at[q, g], device)

    def arrive(q, g):
        ag(q, g, 0, x_peer).wait_recv()

    def x_copy(k, src, dst):
        return rcopy(src, dst, x_send.at[k], x_recv.at[k], x_peer)

    n_links = 3 * nz + chips
    y_link = nz
    c_link = 2 * nz
    sent = []

    def push(q, g, link, device):
        cp = ag(q, g, link, device)
        cp.start()
        sent.append(cp)

    for q in range(chunks):
        for d in hops:
            push(q, own, d, dev(across(d), y, c, x))
        push(q, own, y_link, y_peer)
        push(q, own, c_link, c_peer)
        if q == 0:
            for n, e in enumerate(plane):
                rcopy(gbuf.at[:, gcol(own)], gbuf.at[:, gcol(own)], g_send.at[n], g_recv.at[own],
                      dev(*plane_dev(e), x)).start()
    messages = []

    def x_push(src, dst):
        cp = x_copy(len(messages), src, dst)
        cp.start()
        messages.append(cp)
        return cp

    inv_msg = x_push(inv_s, inv_r)
    hid_msg = [x_push(hs.at[p], hx.at[p, here]) for p in range(PIECES)]
    ct_msg = x_push(cts, ctb.at[here])

    def z_arrivals(q):
        for d in hops:
            g = slot(across(d), y, c)
            arrive(q, g)
            push(q, g, y_link + d, y_peer)
            push(q, g, c_link + d, c_peer)

    def y_arrival(q, d):
        g = slot(across(d), 1 - y, c)
        arrive(q, g)
        push(q, g, c_link + nz + d, c_peer)

    def c_arrivals(q):
        for d in range(nz):
            for yy in (y, 1 - y):
                arrive(q, slot(across(d), yy, 1 - c))

    def norm(which):
        scaled = inv_all[which, :1]
        for p in range(PIECES):
            value = hx[p, which, :].astype(f32) * scaled * gbuf[:, p * lanes : (p + 1) * lanes]
            value = value.astype(bf)
            nbuf[p, which, :] = value
            ntr[p * lanes : (p + 1) * lanes, which] = value.T

    def partial(q):
        out = jnp.zeros((seq, CHUNK), f32)
        for p in range(PIECES):
            w = wbuf[q, p * span : (p + 1) * span].reshape(lanes, CHUNK)
            out = out + nn_dot(nbuf[p], w)
        mix[q] = out

    mycol = pl.ds(pl.multiple_of(x * HD, HD), HD)
    itscol = pl.ds(pl.multiple_of((1 - x) * HD, HD), HD)

    z_arrivals(0)
    for q in range(chunks):
        y_arrival(q, 0)
    for n, e in enumerate(plane):
        g = slot(*plane_dev(e))
        rcopy(gbuf.at[:, gcol(g)], gbuf.at[:, gcol(g)], g_send.at[n], g_recv.at[g], x_peer).wait_recv()
    norm(here)
    z_arrivals(1)
    for d in hops:
        y_arrival(0, d)
    inv_msg.wait_recv()
    for cp in hid_msg:
        cp.wait_recv()
    inv_all[there, :] = jnp.broadcast_to(inv_r[:1, :], (toks, toks)).T
    norm(there)
    c_arrivals(0)
    partial(0)
    kv_s[...] = mix[0].astype(bf)
    kv_msg = x_push(kv_s, kv_r)
    z_arrivals(2)
    q_msg = []
    for n in range(half):
        for d in hops:
            y_arrival(1 + n, d)
        c_arrivals(1 + n)
        partial(1 + n)
        qm_s[n] = mix[1 + n, :, itscol].astype(bf)
        q_msg.append(x_push(qm_s.at[n], qm_r.at[n]))

    loaded(cos_ref, nxt + 3)
    loaded(sin_ref, nxt + 4)
    loaded(ctb.at[here], nxt + 1)
    ct_msg.wait_recv()
    cosine, sine = cos_ref[...], sin_ref[...]

    def rope(u):
        return u * cosine + pltpu.roll(u, HD // 2, 1) * sine

    def unrope(u):
        return u * cosine - pltpu.roll(u, HD // 2, 1) * sine

    kv_msg.wait_recv()
    mix_kv = mix[0] + kv_r[...].astype(f32)
    mix[0] = mix_kv
    keys = rope(mix_kv[:, :HD]).astype(bf)
    values = mix_kv[:, HD:].astype(bf)
    allowed = lax.broadcasted_iota(jnp.int32, (seq, seq), 1) <= lax.broadcasted_iota(jnp.int32, (seq, seq), 0)
    inner = jnp.zeros((seq, 1), f32)
    grad_keys = jnp.zeros((seq, HD), f32)
    grad_values = jnp.zeros((seq, HD), f32)
    gq_msg = []
    for n in range(half):
        q_msg[n].wait_recv()
        mixed = mix[1 + n, :, mycol] + qm_r[n].astype(f32)
        query = (rope(mixed) * scale).astype(bf)
        grad = ctb[:, n * HD : (n + 1) * HD]
        scores = jnp.where(allowed, nt_dot(query, keys), -1e30)
        top = jnp.max(scores, axis=1, keepdims=True)
        numbers = jnp.where(allowed, jnp.exp(scores - top), 0.0)
        norm_sum = jnp.sum(numbers, axis=1, keepdims=True)
        high = numbers.astype(bf)
        low = (numbers - high.astype(f32)).astype(bf)
        attn = ((nn_dot(high, values) + nn_dot(low, values)) / norm_sum).astype(bf)
        at_s[n] = attn
        delta = jnp.sum(grad.astype(f32) * attn.astype(f32), axis=1, keepdims=True)
        probs = numbers / norm_sum
        grad_scores = (probs * (nt_dot(grad, values) - delta)).astype(bf)
        back = (unrope(nn_dot(grad_scores, keys)) * scale).astype(bf)
        gq[n, x] = back
        gq_msg.append(x_push(gq.at[n, x], gq.at[n, x]))
        inner = inner + jnp.sum(back.astype(f32) * mixed, axis=1, keepdims=True)
        grad_keys = grad_keys + tn_dot(grad_scores, query)
        grad_values = grad_values + tn_dot(probs.astype(bf), grad)
    grad_keys = unrope(grad_keys)
    gkv_s[:, :HD] = grad_keys.astype(bf)
    gkv_s[:, HD:] = grad_values.astype(bf)
    gkv_msg = x_push(gkv_s, gkv_r)
    inner_all = jnp.broadcast_to(inner, (seq, HD))
    in_s[...] = inner_all.T[:8, :]
    in_msg = x_push(in_s, in_r)
    for n in range(half):
        attn_ref[:, pl.ds(pl.multiple_of((x * half + n) * HD, HD), HD)] = at_s[n, here, :]

    def to_core(q, k):
        return rcopy(tbuf.at[q, (1 - c) * chips + k], rs1.at[q, k], c_send.at[q, k], c_recv.at[q, k], c_peer)

    def to_y(q, d):
        return rcopy(ybuf.at[q, d], rs2.at[q, d], y_send.at[q, d], y_recv.at[q, d], y_peer)

    def to_z(q, d):
        return rcopy(zbuf.at[q, d - 1], rs3.at[q, d - 1], z_send.at[q, d - 1], z_recv.at[q, d - 1],
                     dev(across(d), y, c, x))

    order = hops[::-1] + [0]

    def term(q, grads, j):
        part = nn_dot(ntr[pl.ds(pl.multiple_of(j * rows, rows), rows), :], grads)
        tbuf[q, j] = part.astype(bf)

    def core_sum(q, k):
        to_core(q, k).wait_recv()
        return tbuf[q, c * chips + k].astype(f32) + rs1[q, k].astype(f32)

    def rs_start(q, grads):
        for yy in (1 - y, y):
            for d in order:
                k = across(d) * SIDE + yy
                term(q, grads, (1 - c) * chips + k)
                to_core(q, k).start()
                term(q, grads, c * chips + k)
        for d in order:
            ybuf[q, d] = core_sum(q, across(d) * SIDE + 1 - y).astype(bf)
            to_y(q, d).start()

    def rs_middle(q):
        for d in order:
            part = core_sum(q, across(d) * SIDE + y)
            to_y(q, d).wait_recv()
            part = part + rs2[q, d].astype(f32)
            if d:
                zbuf[q, d - 1] = part.astype(bf)
                to_z(q, d).start()
            else:
                mix[q, :rows, :] = part

    block = c * chips + z * SIDE + y
    cross = c != x
    sums = []

    def rs_end(q):
        result = mix[q, :rows, :]
        for d in order[:-1]:
            to_z(q, d).wait_recv()
            result = result + rs3[q, d - 1].astype(f32)
        prod = wbuf[q, block].astype(f32) * result
        sums.append(prod[:, :HD] + prod[:, HD:])
        dg_s[q] = result.astype(bf)
        pl.when(cross)(lambda: to_diag(q).start())
        store(q, result)

    def store(q, result):
        if q == 0:
            wg_ref[:, qcols:] = result
        else:
            for xx in range(2):
                first = (xx * half + q - 1) * HD
                wg_ref[:, first : first + HD] = result[:, xx * HD : (xx + 1) * HD]

    def to_diag(q):
        return rcopy(dg_s.at[q], dg_r.at[q], d_send.at[q], d_recv.at[q], d_peer)

    gg_copy = rcopy(gg_s, gg_r, d_send.at[chunks], d_recv.at[chunks], d_peer)

    for n in range(half):
        gq_msg[n].wait_recv()
        rs_start(1 + n, jnp.concatenate([gq[n, 0], gq[n, 1]], axis=1))
    gkv_msg.wait_recv()
    keys_sum = gkv_s[:, :HD].astype(f32) + gkv_r[:, :HD].astype(f32)
    values_sum = gkv_s[:, HD:].astype(f32) + gkv_r[:, HD:].astype(f32)
    gkv_all = jnp.concatenate([keys_sum, values_sum], axis=1).astype(bf)
    gkv[...] = gkv_all
    rs_start(0, gkv_all)
    in_msg.wait_recv()
    inner = inner + jnp.broadcast_to(in_r[:1, :], (HD, seq)).T[:, :1]
    inner = inner + jnp.sum(gkv_all.astype(f32) * mix[0], axis=1, keepdims=True)
    inv = inv_all[...]
    inv_all[...] = inner * (inv * inv / width)
    ntr_inv = inv

    def grad_piece(p, which, scaled):
        out = jnp.zeros((toks, lanes), f32)
        for q in range(chunks):
            w = wbuf[q, p * span : (p + 1) * span].reshape(lanes, CHUNK)
            g = gkv[which, :] if q == 0 else jnp.concatenate([gq[q - 1, 0, which, :], gq[q - 1, 1, which, :]], axis=1)
            out = out + nt_dot(g, w)
        gain = gbuf[:, p * lanes : (p + 1) * lanes]
        return (gain * out * scaled - hx[p, which, :].astype(f32) * inv_all[which, :1]).astype(bf)

    mix[1, :, :HD] = ntr_inv
    gi_msg = []
    for p in range(PIECES):
        gi_s[p] = grad_piece(p, there, mix[1, there, :1])
        gi_msg.append(x_push(gi_s.at[p], gi_r.at[p]))
    at_msg = x_push(at_s.at[:, there], at_r)
    for p in range(PIECES):
        value = grad_piece(p, here, mix[1, here, :1])
        for b in range(span):
            j = p * span + b
            gin_ref[:, pl.ds(pl.multiple_of((2 * j + x) * rows, rows), rows)] = value[:, b * rows : (b + 1) * rows]

    queue = list(range(1, chunks)) + [0]
    rs_middle(queue[0])
    for n in range(1, chunks):
        rs_middle(queue[n])
        rs_end(queue[n - 1])
    rs_end(queue[-1])
    lanes_sum = sums[0]
    for part in sums[1:]:
        lanes_sum = lanes_sum + part
    gg = jnp.sum(lanes_sum.T, axis=0, keepdims=True) / gbuf[:, gcol(block)]
    gg_ref[...] = gg
    gg_s[...] = gg
    pl.when(cross)(lambda: gg_copy.start())

    at_msg.wait_recv()
    for n in range(half):
        attn_ref[:, pl.ds(pl.multiple_of(((1 - x) * half + n) * HD, HD), HD)] = at_r[n]
    for p in range(PIECES):
        gi_msg[p].wait_recv()
        for b in range(span):
            j = p * span + b
            gin_ref[:, pl.ds(pl.multiple_of((2 * j + 1 - x) * rows, rows), rows)] = gi_r[p, :, b * rows : (b + 1) * rows]

    for cp in sent + messages:
        cp.wait_send()
    for n, e in enumerate(plane):
        rcopy(gbuf.at[:, gcol(own)], gbuf.at[:, gcol(own)], g_send.at[n], g_recv.at[own], x_peer).wait_send()
    for q in range(chunks):
        for k in range(chips):
            to_core(q, k).wait_send()
        for d in range(nz):
            to_y(q, d).wait_send()
        for d in hops:
            to_z(q, d).wait_send()

    @pl.when(cross)
    def _():
        for q in queue:
            to_diag(q).wait_recv()
            store(q, dg_r[q].astype(f32))
        gg_copy.wait_recv()
        gg_ref[...] = gg_r[...]
        for q in range(chunks):
            to_diag(q).wait_send()
        gg_copy.wait_send()


def copy_kernel(*refs):
    for k in range(4):
        refs[4 + k][...] = refs[k][...]


def fused(n_inter, hidden_in, norm_gain, qkv_weight, attn_cotangent):
    toks, width = hidden_in.shape[1:]
    rows, cols = qkv_weight.shape
    nz = n_inter // (CORES * SIDE)
    chips = nz * SIDE
    seq, half, chunks = 2 * toks, HEADS // 2, cols // CHUNK
    lanes = n_inter // PIECES * rows
    freqs = rope_base ** (-np.arange(HD // 2, dtype=np.float32) / np.float32(HD // 2))
    angles = (np.arange(seq, dtype=np.float32)[:, None] * freqs.astype(np.float32)[None, :]).astype(np.float32)
    cosine = np.concatenate([np.cos(angles)] * 2, axis=1).astype(np.float32)
    sine = np.concatenate([-np.sin(angles), np.sin(angles)], axis=1).astype(np.float32)
    bf, f32, dma = jnp.bfloat16, jnp.float32, pltpu.SemaphoreType.DMA
    vmem = pl.BlockSpec(memory_space=pltpu.VMEM)
    hbm = pl.BlockSpec(memory_space=pltpu.HBM)
    V = pltpu.VMEM
    n_msgs = 2 * PIECES + 2 * half + 6
    attn, gin, wg, gg = pl.pallas_call(
        functools.partial(fused_kernel, n_inter),
        out_shape=(
            jax.ShapeDtypeStruct((toks, HEADS * HD), bf),
            jax.ShapeDtypeStruct((toks, width), bf),
            jax.ShapeDtypeStruct((rows, cols), f32),
            jax.ShapeDtypeStruct((1, rows), f32),
        ),
        in_specs=[hbm] * 6,
        out_specs=(vmem,) * 4,
        scratch_shapes=[
            V((chunks, n_inter, rows, CHUNK), bf),
            V((1, n_inter * rows), f32),
            V((1, rows), bf),
            V((PIECES, seq, lanes), bf),
            V((PIECES, toks, lanes), bf),
            V((PIECES, seq, lanes), bf),
            V((n_inter * rows, seq), bf),
            V((seq, HD), f32),
            V((8, toks), f32),
            V((8, toks), f32),
            V((seq, half * HD), bf),
            V((toks, half * HD), bf),
            V((seq, HD), f32),
            V((seq, HD), f32),
            V((chunks, seq, CHUNK), f32),
            V((seq, CHUNK), bf),
            V((seq, CHUNK), bf),
            V((half, seq, HD), bf),
            V((half, seq, HD), bf),
            V((half, 2, seq, HD), bf),
            V((seq, CHUNK), bf),
            V((seq, CHUNK), bf),
            V((seq, CHUNK), bf),
            V((8, seq), f32),
            V((8, seq), f32),
            V((half, seq, HD), bf),
            V((half, toks, HD), bf),
            V((PIECES, toks, lanes), bf),
            V((PIECES, toks, lanes), bf),
            V((chunks, n_inter, rows, CHUNK), bf),
            V((chunks, chips, rows, CHUNK), bf),
            V((chunks, nz, rows, CHUNK), bf),
            V((chunks, nz, rows, CHUNK), bf),
            V((chunks, nz - 1, rows, CHUNK), bf),
            V((chunks, nz - 1, rows, CHUNK), bf),
            V((chunks, rows, CHUNK), bf),
            V((chunks, rows, CHUNK), bf),
            V((1, rows), f32),
            V((1, rows), f32),
            dma((8 + half,)),
            dma((chunks, 2 * nz + chips)), dma((chunks, n_inter)),
            dma((n_inter,)), dma((n_inter,)),
            dma((n_msgs,)), dma((n_msgs,)),
            dma((chunks, chips)), dma((chunks, chips)),
            dma((chunks, nz)), dma((chunks, nz)),
            dma((chunks, nz - 1)), dma((chunks, nz - 1)),
            dma((chunks + 1,)), dma((chunks + 1,)),
        ],
        compiler_params=pltpu.CompilerParams(
            collective_id=0, has_side_effects=True, vmem_limit_bytes=32 * 2**20
        ),
    )(hidden_in[0], norm_gain[None], qkv_weight, attn_cotangent[0], cosine, sine)
    outs = (attn, gin, wg, gg)
    attn, gin, wg, gg = pl.pallas_call(
        copy_kernel,
        out_shape=tuple(jax.ShapeDtypeStruct(o.shape, o.dtype) for o in outs),
        in_specs=[vmem] * 4,
        out_specs=(vmem,) * 4,
    )(*outs)
    return attn[None], gin[None], wg, gg[0]


def solution(mesh):
    n_inter, n_intra = mesh.shape["inter"], mesh.shape["intra"]

    def body(hidden_in, norm_gain, qkv_weight, attn_cotangent):
        nz = n_inter // (CORES * SIDE)
        fits = n_intra == 2 and n_inter % (CORES * SIDE) == 0 and nz > 1 and nz & (nz - 1) == 0
        fits = fits and qkv_weight.shape[0] == HD and hidden_in.shape[0] == 1
        fits = fits and hidden_in.shape[1] == HD and n_inter % PIECES == 0
        if fits:
            return fused(n_inter, hidden_in, norm_gain, qkv_weight, attn_cotangent)
        return local(hidden_in, norm_gain, qkv_weight, attn_cotangent)

    return jax.shard_map(
        body,
        mesh=mesh,
        in_specs=(
            P("inter", "intra", None),
            P(("inter", "intra")),
            P(("inter", "intra"), None),
            P("inter", "intra", None),
        ),
        out_specs=(
            P("inter", "intra", None),
            P("inter", "intra", None),
            P(("intra", "inter"), None),
            P(("intra", "inter")),
        ),
        check_vma=False,
    )
```

time: 95 us -> 81.3 us (0.86)
  the two profiles are of different devices: /device:TPU:0 before, /device:TPU:1 now
where the time goes in v1:
time: 81.3 us; the launch traced here: 81 us
  Pallas kernels  72 us (89%)
  local copies, waits for them, and re-layouts  8.42 us (10%)
    pallas_call x1, Pallas kernels, fused(): pl.pallas_call(functools.partial(fused_kernel, n_inter), out_shape=(jax.S...  69.4 us
    unnamed x20, local copies, waits for them, and re-layouts  8.42 us
    pallas_call x1, Pallas kernels, fused(): pl.pallas_call(copy_kernel, out_shape=tuple((jax.ShapeDtypeStruct(o.shape...  2.56 us

profile of v1, /device:TPU:1, one launch (start us, length us, event | category | flops | bytes accessed | tf_op | source)
XLA Modules:
  0.0 81.0 jit_solution(12325595828528609424)
XLA Ops:
  0.6 0.0 copy-start.8
  0.6 0.6 copy-done.8
  1.3 0.0 copy-start
  1.3 1.2 %copy-done = bf16[1,128,4096]{2,1,0:T(8,128)(2,1)S(1)} copy-done((bf16[1,128,4096]{2,1,0:T(8,128)(2,1)S(1)}, bf16[1,128,4096]{2,1,0:T(8,128)(2,1)}, u32[]{:S(2)}) %copy-start) | copy-done | bytes 1048600
  2.5 0.0 copy-start.3
  2.5 0.9 %copy-done.3 = bf16[128,768]{1,0:T(8,128)(2,1)S(1)} copy-done((bf16[128,768]{1,0:T(8,128)(2,1)S(1)}, bf16[128,768]{1,0:T(8,128)(2,1)}, u32[]{:S(2)}) %copy-start.3) | copy-done | bytes 196632
  3.4 0.0 copy-start.4
  3.4 0.9 %copy-done.4 = bf16[1,128,512]{2,1,0:T(8,128)(2,1)S(1)} copy-done((bf16[1,128,512]{2,1,0:T(8,128)(2,1)S(1)}, bf16[1,128,512]{2,1,0:T(8,128)(2,1)}, u32[]{:S(2)}) %copy-start.4) | copy-done | bytes 131096
  4.3 0.0 copy-start.6
  4.3 0.9 %copy-done.6 = f32[256,128]{1,0:T(8,128)S(1)} copy-done((f32[256,128]{1,0:T(8,128)S(1)}, f32[256,128]{1,0:T(8,128)}, u32[]{:S(2)}) %copy-start.6) | copy-done | bytes 131096
  5.2 0.0 copy-start.7
  5.3 0.9 %copy-done.7 = f32[256,128]{1,0:T(8,128)S(1)} copy-done((f32[256,128]{1,0:T(8,128)S(1)}, f32[256,128]{1,0:T(8,128)}, u32[]{:S(2)}) %copy-start.7) | copy-done | bytes 131096
  6.2 69.4 %shard_map.93 = (bf16[128,512]{1,0:T(8,128)(2,1)S(1)}, bf16[128,4096]{1,0:T(8,128)(2,1)S(1)}, f32[128,768]{1,0:T(8,128)S(1)}, f32[1,128]{1,0:T(1,128)S(1)}) custom-call(bf16[128,4096]{1,0:T(8,128)(2,1)S(1)} %bitcast.6, bf16[1,128]{1,0:T(2,128)(2,1)S(1)} %bitcast.8, bf16[128,768]{1,0:T(8,128)(2,1)S(1)} %copy-done.3, bf16[128,512]{1,0:T(8,128)(2,1)S(1)} %bitcast.7, ...), custom_call_target="tpu_custom_call" | custom-call | tf_op jit(solution)/shard_map/pallas_call | solution.py:694
  75.6 0.0 copy-start.1
  75.6 1.0 %copy-done.1 = bf16[128,4096]{1,0:T(8,128)(2,1)} copy-done((bf16[128,4096]{1,0:T(8,128)(2,1)}, bf16[128,4096]{1,0:T(8,128)(2,1)S(1)}, u32[]{:S(2)}) %copy-start.1) | copy-done | bytes 1048600
  76.5 0.0 copy-start.2
  76.5 0.8 copy-done.2
  77.3 0.0 copy-start.5
  77.3 0.6 copy-done.5
  77.9 0.0 copy-start.9
  77.9 0.5 copy-done.9
  78.5 2.6 %shard_map.94 = (bf16[128,512]{1,0:T(8,128)(2,1)}, bf16[128,4096]{1,0:T(8,128)(2,1)}, f32[128,768]{1,0:T(8,128)}, f32[1,128]{1,0:T(1,128)}) custom-call(bf16[128,512]{1,0:T(8,128)(2,1)} %copy-done.5, bf16[128,4096]{1,0:T(8,128)(2,1)} %copy-done.1, f32[128,768]{1,0:T(8,128)} %copy-done.2, f32[1,128]{1,0:T(1,128)} %copy-done.9), custom_call_target="tpu_custom_call" | custom-call | tf_op jit(solution)/shard_map/pallas_call | solution.py:758
Async XLA Ops:
  0.6 0.7 copy-start.8
  1.3 1.2 %copy-start = (bf16[1,128,4096]{2,1,0:T(8,128)(2,1)S(1)}, bf16[1,128,4096]{2,1,0:T(8,128)(2,1)}, u32[]{:S(2)}) copy-start(bf16[1,128,4096]{2,1,0:T(8,128)(2,1)} %param.6) | copy-start | bytes 3145732
  2.5 0.9 %copy-start.3 = (bf16[128,768]{1,0:T(8,128)(2,1)S(1)}, bf16[128,768]{1,0:T(8,128)(2,1)}, u32[]{:S(2)}) copy-start(bf16[128,768]{1,0:T(8,128)(2,1)} %w_ref.1) | copy-start | bytes 589828
  3.4 0.9 %copy-start.4 = (bf16[1,128,512]{2,1,0:T(8,128)(2,1)S(1)}, bf16[1,128,512]{2,1,0:T(8,128)(2,1)}, u32[]{:S(2)}) copy-start(bf16[1,128,512]{2,1,0:T(8,128)(2,1)} %param.9) | copy-start | bytes 393220
  4.3 0.9 %copy-start.6 = (f32[256,128]{1,0:T(8,128)S(1)}, f32[256,128]{1,0:T(8,128)}, u32[]{:S(2)}) copy-start(f32[256,128]{1,0:T(8,128)} %constant.5.clone.sin_hbm) | copy-start | bytes 393220
  5.2 0.9 %copy-start.7 = (f32[256,128]{1,0:T(8,128)S(1)}, f32[256,128]{1,0:T(8,128)}, u32[]{:S(2)}) copy-start(f32[256,128]{1,0:T(8,128)} %constant.4.clone.cos_hbm) | copy-start | bytes 393220
  75.6 1.0 %copy-start.1 = (bf16[128,4096]{1,0:T(8,128)(2,1)}, bf16[128,4096]{1,0:T(8,128)(2,1)S(1)}, u32[]{:S(2)}) copy-start(bf16[128,4096]{1,0:T(8,128)(2,1)S(1)} %get-tuple-element.13.refs_1_) | copy-start | bytes 3145732
  76.5 0.8 copy-start.2
  77.3 0.6 copy-start.5
  77.9 0.5 copy-start.9

commit v2 on v1

--- a/solution.py
+++ b/solution.py
@@ -253,10 +253,10 @@
     hid_ref, gain_ref, w_ref, ct_ref, cos_hbm, sin_hbm,
     attn_ref, gin_ref, wg_ref, gg_ref,
     wbuf, gbuf, gain_in, hx, hs, nbuf, ntr, inv_all, inv_s, inv_r, ctb, cts, cos_ref, sin_ref,
-    mix, kv_s, kv_r, qm_s, qm_r, gq, gkv_s, gkv_r, gkv, in_s, in_r, at_s, at_r, gi_s, gi_r,
-    tbuf, rs1, ybuf, rs2, zbuf, rs3, dg_s, dg_r, gg_s, gg_r,
+    mix, kv_s, kv_r, qm_s, qm_r, gq, gkv_s, gkv_r, in_s, in_r, at_s, at_r, gi_s, gi_r,
+    tbuf, rs1, ybuf, rs2, zbuf, rs3, side, dg_s, dg_r, gg_s, gg_r,
     ld_sem, ag_send, ag_recv, g_send, g_recv, x_send, x_recv,
-    c_send, c_recv, y_send, y_recv, z_send, z_recv, d_send, d_recv,
+    c_send, c_recv, y_send, y_recv, z_send, z_recv, s_send, s_recv, d_send, d_recv,
 ):
     i = lax.axis_index("inter")
     x = lax.axis_index("intra")
@@ -358,6 +358,10 @@
     loaded(cts, nxt + 2)
     pl.semaphore_wait(barrier, len(peers))
 
+    inner_z = jnp.logical_and(z > 0, z < nz - 1)
+    far = nz - 1 if nz > 2 else None
+    spare = chunks - 1
+
     def ag(q, g, link, device):
         return rcopy(wbuf.at[q, g], wbuf.at[q, g], ag_send.at[q, link], ag_recv.at[q, g], device)
 
@@ -367,25 +371,27 @@
     def x_copy(k, src, dst):
         return rcopy(src, dst, x_send.at[k], x_recv.at[k], x_peer)
 
-    n_links = 3 * nz + chips
     y_link = nz
     c_link = 2 * nz
+    spare_link = 2 * nz + chips
     sent = []
 
-    def push(q, g, link, device):
+    def push(q, g, link, device, cond=None):
         cp = ag(q, g, link, device)
-        cp.start()
-        sent.append(cp)
-
+        sent.append((cp, cond))
+        if cond is None:
+            cp.start()
+        else:
+            pl.when(cond)(cp.start)
+
+    for n, e in enumerate(plane):
+        rcopy(gbuf.at[:, gcol(own)], gbuf.at[:, gcol(own)], g_send.at[n], g_recv.at[own],
+              dev(*plane_dev(e), x)).start()
     for q in range(chunks):
-        for d in hops:
-            push(q, own, d, dev(across(d), y, c, x))
+        for d in sorted(hops, key=lambda d: d % 2):
+            push(q, own, d, dev(across(d), y, c, x), inner_z if d == far else None)
         push(q, own, y_link, y_peer)
         push(q, own, c_link, c_peer)
-        if q == 0:
-            for n, e in enumerate(plane):
-                rcopy(gbuf.at[:, gcol(own)], gbuf.at[:, gcol(own)], g_send.at[n], g_recv.at[own],
-                      dev(*plane_dev(e), x)).start()
     messages = []
 
     def x_push(src, dst):
@@ -402,12 +408,17 @@
         for d in hops:
             g = slot(across(d), y, c)
             arrive(q, g)
-            push(q, g, y_link + d, y_peer)
+            if d == 2:
+                push(q, g, 0, dev(across(1), y, c, x), inner_z)
+            if q != spare or d != 1:
+                push(q, g, y_link + d, y_peer)
             push(q, g, c_link + d, c_peer)
 
     def y_arrival(q, d):
         g = slot(across(d), 1 - y, c)
         arrive(q, g)
+        if q == spare and d == 0:
+            push(q, g, spare_link, dev(across(1), y, c, x))
         push(q, g, c_link + nz + d, c_peer)
 
     def c_arrivals(q):
@@ -436,11 +447,11 @@
     z_arrivals(0)
     for q in range(chunks):
         y_arrival(q, 0)
+    z_arrivals(1)
     for n, e in enumerate(plane):
         g = slot(*plane_dev(e))
         rcopy(gbuf.at[:, gcol(g)], gbuf.at[:, gcol(g)], g_send.at[n], g_recv.at[g], x_peer).wait_recv()
     norm(here)
-    z_arrivals(1)
     for d in hops:
         y_arrival(0, d)
     inv_msg.wait_recv()
@@ -484,7 +495,8 @@
     grad_keys = jnp.zeros((seq, HD), f32)
     grad_values = jnp.zeros((seq, HD), f32)
     gq_msg = []
-    for n in range(half):
+
+    def head(n, inner, grad_keys, grad_values):
         q_msg[n].wait_recv()
         mixed = mix[1 + n, :, mycol] + qm_r[n].astype(f32)
         query = (rope(mixed) * scale).astype(bf)
@@ -506,6 +518,110 @@
         inner = inner + jnp.sum(back.astype(f32) * mixed, axis=1, keepdims=True)
         grad_keys = grad_keys + tn_dot(grad_scores, query)
         grad_values = grad_values + tn_dot(probs.astype(bf), grad)
+        return inner, grad_keys, grad_values
+
+    def to_core(q, k):
+        return rcopy(tbuf.at[q, (1 - c) * chips + k], rs1.at[q, k], c_send.at[q, k], c_recv.at[q, k], c_peer)
+
+    def to_y(q, d):
+        return rcopy(ybuf.at[q, d], rs2.at[q, d], y_send.at[q, d], y_recv.at[q, d], y_peer)
+
+    def to_z(q, d):
+        return rcopy(zbuf.at[q, d - 1], rs3.at[q, d - 1], z_send.at[q, d - 1], z_recv.at[q, d - 1],
+                     dev(across(d), y, c, x))
+
+    order = ([far] if far else []) + hops[:far - 1 if far else None] + [0]
+    turn = chunks - 1
+
+    def terms(q, grads, cc):
+        part = nn_dot(ntr[pl.ds(pl.multiple_of(cc * chips * rows, rows), chips * rows), :], grads)
+        tbuf[q, pl.ds(cc * chips, chips)] = part.astype(bf).reshape(chips, rows, CHUNK)
+
+    def to_side(q, k, src):
+        return rcopy(src, side.at[k, q], s_send.at[k, q], s_recv.at[k, q], dev(across(1), y, c, x))
+
+    def core_sum(q, k):
+        to_core(q, k).wait_recv()
+        return tbuf[q, c * chips + k].astype(f32) + rs1[q, k].astype(f32)
+
+    def rs_start(q, grads):
+        terms(q, grads, 1 - c)
+        for yy in (1 - y, y):
+            for d in order:
+                to_core(q, across(d) * SIDE + yy).start()
+        terms(q, grads, c)
+        for d in order:
+            part = core_sum(q, across(d) * SIDE + 1 - y)
+            if q == turn and d == 0:
+                to_side(q, 0, ybuf.at[q, 1]).wait_recv()
+                part = part + side[0, q].astype(f32)
+            ybuf[q, d] = part.astype(bf)
+            if q == turn and d == 1:
+                to_side(q, 0, ybuf.at[q, d]).start()
+            else:
+                to_y(q, d).start()
+
+    def rs_middle(q):
+        for d in order:
+            part = core_sum(q, across(d) * SIDE + y)
+            if q != turn or d != 1:
+                to_y(q, d).wait_recv()
+                part = part + rs2[q, d].astype(f32)
+            if d == 0:
+                mix[q, :rows, :] = part
+            elif d == far:
+                zbuf[q, d - 1] = part.astype(bf)
+                pl.when(inner_z)(to_z(q, d).start)
+                pl.when(jnp.logical_not(inner_z))(to_side(q, 1, zbuf.at[q, d - 1]).start)
+            elif d == 2:
+                pl.when(inner_z)(to_side(q, 1, zbuf.at[q, d - 1]).wait_recv)
+                extra = jnp.where(inner_z, side[1, q].astype(f32), 0.0)
+                zbuf[q, d - 1] = (part + extra).astype(bf)
+                to_z(q, d).start()
+            else:
+                zbuf[q, d - 1] = part.astype(bf)
+                to_z(q, d).start()
+
+    block = c * chips + z * SIDE + y
+    cross = c != x
+    sums = []
+
+    def rs_end(q):
+        result = mix[q, :rows, :]
+        for d in hops:
+            if d == far:
+                pl.when(inner_z)(to_z(q, d).wait_recv)
+                result = result + jnp.where(inner_z, rs3[q, d - 1].astype(f32), 0.0)
+            else:
+                to_z(q, d).wait_recv()
+                result = result + rs3[q, d - 1].astype(f32)
+        prod = wbuf[q, block].astype(f32) * result
+        sums.append(prod[:, :HD] + prod[:, HD:])
+        dg_s[q] = result.astype(bf)
+        pl.when(cross)(lambda: to_diag(q).start())
+        store(q, result)
+
+    def store(q, result):
+        if q == 0:
+            wg_ref[:, qcols:] = result
+        else:
+            for xx in range(2):
+                first = (xx * half + q - 1) * HD
+                wg_ref[:, first : first + HD] = result[:, xx * HD : (xx + 1) * HD]
+
+    def to_diag(q):
+        return rcopy(dg_s.at[q], dg_r.at[q], d_send.at[q], d_recv.at[q], d_peer)
+
+    gg_copy = rcopy(gg_s, gg_r, d_send.at[chunks], d_recv.at[chunks], d_peer)
+
+    def rs_head(n):
+        gq_msg[n].wait_recv()
+        rs_start(1 + n, jnp.concatenate([gq[n, 0], gq[n, 1]], axis=1))
+
+    for n in range(half):
+        inner, grad_keys, grad_values = head(n, inner, grad_keys, grad_values)
+        if n < half - 1:
+            rs_head(n)
     grad_keys = unrope(grad_keys)
     gkv_s[:, :HD] = grad_keys.astype(bf)
     gkv_s[:, HD:] = grad_values.astype(bf)
@@ -516,115 +632,36 @@
     for n in range(half):
         attn_ref[:, pl.ds(pl.multiple_of((x * half + n) * HD, HD), HD)] = at_s[n, here, :]
 
-    def to_core(q, k):
-        return rcopy(tbuf.at[q, (1 - c) * chips + k], rs1.at[q, k], c_send.at[q, k], c_recv.at[q, k], c_peer)
-
-    def to_y(q, d):
-        return rcopy(ybuf.at[q, d], rs2.at[q, d], y_send.at[q, d], y_recv.at[q, d], y_peer)
-
-    def to_z(q, d):
-        return rcopy(zbuf.at[q, d - 1], rs3.at[q, d - 1], z_send.at[q, d - 1], z_recv.at[q, d - 1],
-                     dev(across(d), y, c, x))
-
-    order = hops[::-1] + [0]
-
-    def term(q, grads, j):
-        part = nn_dot(ntr[pl.ds(pl.multiple_of(j * rows, rows), rows), :], grads)
-        tbuf[q, j] = part.astype(bf)
-
-    def core_sum(q, k):
-        to_core(q, k).wait_recv()
-        return tbuf[q, c * chips + k].astype(f32) + rs1[q, k].astype(f32)
-
-    def rs_start(q, grads):
-        for yy in (1 - y, y):
-            for d in order:
-                k = across(d) * SIDE + yy
-                term(q, grads, (1 - c) * chips + k)
-                to_core(q, k).start()
-                term(q, grads, c * chips + k)
-        for d in order:
-            ybuf[q, d] = core_sum(q, across(d) * SIDE + 1 - y).astype(bf)
-            to_y(q, d).start()
-
-    def rs_middle(q):
-        for d in order:
-            part = core_sum(q, across(d) * SIDE + y)
-            to_y(q, d).wait_recv()
-            part = part + rs2[q, d].astype(f32)
-            if d:
-                zbuf[q, d - 1] = part.astype(bf)
-                to_z(q, d).start()
-            else:
-                mix[q, :rows, :] = part
-
-    block = c * chips + z * SIDE + y
-    cross = c != x
-    sums = []
-
-    def rs_end(q):
-        result = mix[q, :rows, :]
-        for d in order[:-1]:
-            to_z(q, d).wait_recv()
-            result = result + rs3[q, d - 1].astype(f32)
-        prod = wbuf[q, block].astype(f32) * result
-        sums.append(prod[:, :HD] + prod[:, HD:])
-        dg_s[q] = result.astype(bf)
-        pl.when(cross)(lambda: to_diag(q).start())
-        store(q, result)
-
-    def store(q, result):
-        if q == 0:
-            wg_ref[:, qcols:] = result
-        else:
-            for xx in range(2):
-                first = (xx * half + q - 1) * HD
-                wg_ref[:, first : first + HD] = result[:, xx * HD : (xx + 1) * HD]
-
-    def to_diag(q):
-        return rcopy(dg_s.at[q], dg_r.at[q], d_send.at[q], d_recv.at[q], d_peer)
-
-    gg_copy = rcopy(gg_s, gg_r, d_send.at[chunks], d_recv.at[chunks], d_peer)
-
-    for n in range(half):
-        gq_msg[n].wait_recv()
-        rs_start(1 + n, jnp.concatenate([gq[n, 0], gq[n, 1]], axis=1))
+    rs_head(half - 1)
     gkv_msg.wait_recv()
     keys_sum = gkv_s[:, :HD].astype(f32) + gkv_r[:, :HD].astype(f32)
     values_sum = gkv_s[:, HD:].astype(f32) + gkv_r[:, HD:].astype(f32)
     gkv_all = jnp.concatenate([keys_sum, values_sum], axis=1).astype(bf)
-    gkv[...] = gkv_all
     rs_start(0, gkv_all)
     in_msg.wait_recv()
     inner = inner + jnp.broadcast_to(in_r[:1, :], (HD, seq)).T[:, :1]
     inner = inner + jnp.sum(gkv_all.astype(f32) * mix[0], axis=1, keepdims=True)
     inv = inv_all[...]
     inv_all[...] = inner * (inv * inv / width)
-    ntr_inv = inv
-
-    def grad_piece(p, which, scaled):
-        out = jnp.zeros((toks, lanes), f32)
+
+    gqs = [jnp.concatenate([gq[n, 0], gq[n, 1]], axis=1) for n in range(half)]
+    gi_msg = []
+    for p in range(PIECES):
+        out = jnp.zeros((seq, lanes), f32)
         for q in range(chunks):
             w = wbuf[q, p * span : (p + 1) * span].reshape(lanes, CHUNK)
-            g = gkv[which, :] if q == 0 else jnp.concatenate([gq[q - 1, 0, which, :], gq[q - 1, 1, which, :]], axis=1)
-            out = out + nt_dot(g, w)
+            out = out + nt_dot(gkv_all if q == 0 else gqs[q - 1], w)
         gain = gbuf[:, p * lanes : (p + 1) * lanes]
-        return (gain * out * scaled - hx[p, which, :].astype(f32) * inv_all[which, :1]).astype(bf)
-
-    mix[1, :, :HD] = ntr_inv
-    gi_msg = []
+        gi_s[p] = (gain * out * inv[:, :1] - hx[p].astype(f32) * inv_all[:, :1]).astype(bf)
+        gi_msg.append(x_push(gi_s.at[p, there], gi_r.at[p]))
+    at_msg = x_push(at_s.at[:, there], at_r)
+
+    queue = list(range(1, chunks)) + [0]
+    rs_middle(queue[0])
     for p in range(PIECES):
-        gi_s[p] = grad_piece(p, there, mix[1, there, :1])
-        gi_msg.append(x_push(gi_s.at[p], gi_r.at[p]))
-    at_msg = x_push(at_s.at[:, there], at_r)
-    for p in range(PIECES):
-        value = grad_piece(p, here, mix[1, here, :1])
         for b in range(span):
             j = p * span + b
-            gin_ref[:, pl.ds(pl.multiple_of((2 * j + x) * rows, rows), rows)] = value[:, b * rows : (b + 1) * rows]
-
-    queue = list(range(1, chunks)) + [0]
-    rs_middle(queue[0])
+            gin_ref[:, pl.ds(pl.multiple_of((2 * j + x) * rows, rows), rows)] = gi_s[p, here, b * rows : (b + 1) * rows]
     for n in range(1, chunks):
         rs_middle(queue[n])
         rs_end(queue[n - 1])
@@ -646,7 +683,12 @@
             j = p * span + b
             gin_ref[:, pl.ds(pl.multiple_of((2 * j + 1 - x) * rows, rows), rows)] = gi_r[p, :, b * rows : (b + 1) * rows]
 
-    for cp in sent + messages:
+    for cp, cond in sent:
+        if cond is None:
+            cp.wait_send()
+        else:
+            pl.when(cond)(cp.wait_send)
+    for cp in messages:
         cp.wait_send()
     for n, e in enumerate(plane):
         rcopy(gbuf.at[:, gcol(own)], gbuf.at[:, gcol(own)], g_send.at[n], g_recv.at[own], x_peer).wait_send()
@@ -654,9 +696,16 @@
         for k in range(chips):
             to_core(q, k).wait_send()
         for d in range(nz):
-            to_y(q, d).wait_send()
+            if q != turn or d != 1:
+                to_y(q, d).wait_send()
+            else:
+                to_side(q, 0, ybuf.at[q, d]).wait_send()
         for d in hops:
-            to_z(q, d).wait_send()
+            if d == far:
+                pl.when(inner_z)(to_z(q, d).wait_send)
+                pl.when(jnp.logical_not(inner_z))(to_side(q, 1, zbuf.at[q, d - 1]).wait_send)
+            else:
+                to_z(q, d).wait_send()
 
     @pl.when(cross)
     def _():
@@ -671,8 +720,12 @@
 
 
 def copy_kernel(*refs):
-    for k in range(4):
-        refs[4 + k][...] = refs[k][...]
+    sems = refs[8]
+    copies = [pltpu.make_async_copy(refs[k], refs[4 + k], sems.at[k]) for k in range(4)]
+    for cp in copies:
+        cp.start()
+    for cp in copies:
+        cp.wait()
 
 
 def fused(n_inter, hidden_in, norm_gain, qkv_weight, attn_cotangent):
@@ -691,14 +744,10 @@
     hbm = pl.BlockSpec(memory_space=pltpu.HBM)
     V = pltpu.VMEM
     n_msgs = 2 * PIECES + 2 * half + 6
+    ins = (hidden_in[0], norm_gain[None], qkv_weight, attn_cotangent[0], jnp.asarray(cosine), jnp.asarray(sine))
     attn, gin, wg, gg = pl.pallas_call(
         functools.partial(fused_kernel, n_inter),
-        out_shape=(
-            jax.ShapeDtypeStruct((toks, HEADS * HD), bf),
-            jax.ShapeDtypeStruct((toks, width), bf),
-            jax.ShapeDtypeStruct((rows, cols), f32),
-            jax.ShapeDtypeStruct((1, rows), f32),
-        ),
+        out_shape=(V((toks, HEADS * HD), bf), V((toks, width), bf), V((rows, cols), f32), V((1, rows), f32)),
         in_specs=[hbm] * 6,
         out_specs=(vmem,) * 4,
         scratch_shapes=[
@@ -724,12 +773,11 @@
             V((half, 2, seq, HD), bf),
             V((seq, CHUNK), bf),
             V((seq, CHUNK), bf),
-            V((seq, CHUNK), bf),
             V((8, seq), f32),
             V((8, seq), f32),
             V((half, seq, HD), bf),
             V((half, toks, HD), bf),
-            V((PIECES, toks, lanes), bf),
+            V((PIECES, seq, lanes), bf),
             V((PIECES, toks, lanes), bf),
             V((chunks, n_inter, rows, CHUNK), bf),
             V((chunks, chips, rows, CHUNK), bf),
@@ -737,30 +785,34 @@
             V((chunks, nz, rows, CHUNK), bf),
             V((chunks, nz - 1, rows, CHUNK), bf),
             V((chunks, nz - 1, rows, CHUNK), bf),
+            V((2, chunks, rows, CHUNK), bf),
             V((chunks, rows, CHUNK), bf),
             V((chunks, rows, CHUNK), bf),
             V((1, rows), f32),
             V((1, rows), f32),
             dma((8 + half,)),
-            dma((chunks, 2 * nz + chips)), dma((chunks, n_inter)),
+            dma((chunks, 2 * nz + chips + 1)), dma((chunks, n_inter)),
             dma((n_inter,)), dma((n_inter,)),
             dma((n_msgs,)), dma((n_msgs,)),
             dma((chunks, chips)), dma((chunks, chips)),
             dma((chunks, nz)), dma((chunks, nz)),
             dma((chunks, nz - 1)), dma((chunks, nz - 1)),
+            dma((2, chunks)), dma((2, chunks)),
             dma((chunks + 1,)), dma((chunks + 1,)),
         ],
         compiler_params=pltpu.CompilerParams(
             collective_id=0, has_side_effects=True, vmem_limit_bytes=32 * 2**20
         ),
-    )(hidden_in[0], norm_gain[None], qkv_weight, attn_cotangent[0], cosine, sine)
+    )(*[pltpu.with_memory_space_constraint(a, pltpu.HBM) for a in ins])
     outs = (attn, gin, wg, gg)
     attn, gin, wg, gg = pl.pallas_call(
         copy_kernel,
         out_shape=tuple(jax.ShapeDtypeStruct(o.shape, o.dtype) for o in outs),
         in_specs=[vmem] * 4,
-        out_specs=(vmem,) * 4,
-    )(*outs)
+        out_specs=(hbm,) * 4,
+        scratch_shapes=[dma((4,))],
+        compiler_params=pltpu.CompilerParams(vmem_limit_bytes=2**20),
+    )(*[pltpu.with_memory_space_constraint(o, pltpu.VMEM) for o in outs])
     return attn[None], gin[None], wg, gg[0]
 
 

time: 81.3 us -> 70.5 us (0.87)
  local copies, waits for them, and re-layouts: 8.42 us -> 0 us
  Pallas kernels: 72 us -> 69.7 us
    unnamed x20 -> x0, local copies, waits for them, and re-layouts: 8.42 us -> none
    pallas_call x1, Pallas kernels: 2.56 us -> 1.17 us  [fused(): pl.pallas_call(copy_kernel, out_shape=tuple((jax.ShapeDtypeStruct(o.shape...]
    pallas_call x1, Pallas kernels: 69.4 us -> 68.5 us  [fused(): pl.pallas_call(functools.partial(fused_kernel, n_inter), out_shape=(V((to...]
where the time goes in v2:
time: 70.5 us; the launch traced here: 70.3 us
  Pallas kernels  69.7 us (99%)
    pallas_call x1, Pallas kernels, fused(): pl.pallas_call(functools.partial(fused_kernel, n_inter), out_shape=(V((to...  68.5 us

profile of v2, /device:TPU:1, one launch (start us, length us, event | category | flops | bytes accessed | tf_op | source)
XLA Modules:
  0.0 70.3 jit_solution(13577395393672967236)
XLA Ops:
  0.6 68.5 %shard_map.93 = (bf16[128,512]{1,0:T(8,128)(2,1)S(1)}, bf16[128,4096]{1,0:T(8,128)(2,1)S(1)}, f32[128,768]{1,0:T(8,128)S(1)}, f32[1,128]{1,0:T(1,128)S(1)}) custom-call(bf16[128,4096]{1,0:T(8,128)(2,1)} %bitcast.6, bf16[1,128]{1,0:T(2,128)(2,1)} %bitcast.8, bf16[128,768]{1,0:T(8,128)(2,1)} %w_ref.1, bf16[128,512]{1,0:T(8,128)(2,1)} %bitcast.7, ...), custom_call_target="tpu_custom_call" | custom-call | tf_op jit(solution)/shard_map/pallas_call | solution.py:748
  69.2 1.2 %shard_map.94 = (bf16[128,512]{1,0:T(8,128)(2,1)}, bf16[128,4096]{1,0:T(8,128)(2,1)}, f32[128,768]{1,0:T(8,128)}, f32[1,128]{1,0:T(1,128)}) custom-call(bf16[128,512]{1,0:T(8,128)(2,1)S(1)} %get-tuple-element.12.refs_0_, bf16[128,4096]{1,0:T(8,128)(2,1)S(1)} %get-tuple-element.13.refs_1_, f32[128,768]{1,0:T(8,128)S(1)} %get-tuple-element.14.refs_2_, ...), custom_call_target="tpu_custom_call" | custom-call | tf_op jit(solution)/shard_map/pallas_call | solution.py:808

commit v3 on v2

--- a/solution.py
+++ b/solution.py
@@ -387,9 +387,13 @@
     for n, e in enumerate(plane):
         rcopy(gbuf.at[:, gcol(own)], gbuf.at[:, gcol(own)], g_send.at[n], g_recv.at[own],
               dev(*plane_dev(e), x)).start()
+    def own_z(q):
+        for d in ([far] if far else []) + hops[::-1][1 if far else 0 :]:
+            push(q, own, d, dev(across(d), y, c, x), inner_z if d == far and q else None)
+
     for q in range(chunks):
-        for d in sorted(hops, key=lambda d: d % 2):
-            push(q, own, d, dev(across(d), y, c, x), inner_z if d == far else None)
+        if q < chunks - 1:
+            own_z(q)
         push(q, own, y_link, y_peer)
         push(q, own, c_link, c_peer)
     messages = []
@@ -404,18 +408,26 @@
     hid_msg = [x_push(hs.at[p], hx.at[p, here]) for p in range(PIECES)]
     ct_msg = x_push(cts, ctb.at[here])
 
-    def z_arrivals(q):
-        for d in hops:
-            g = slot(across(d), y, c)
-            arrive(q, g)
-            if d == 2:
-                push(q, g, 0, dev(across(1), y, c, x), inner_z)
-            if q != spare or d != 1:
-                push(q, g, y_link + d, y_peer)
-            push(q, g, c_link + d, c_peer)
+    def near(n):
+        if n < 2:
+            return across(n)
+        return jnp.where(inner_z, across(nz + 1 - n), across(n))
+
+    def z_arrival(q, n):
+        g = slot(near(n), y, c)
+        arrive(q, g)
+        if n == far and q:
+            push(q, g, 0, dev(across(1), y, c, x), inner_z)
+        if q != spare or n != 1:
+            push(q, g, y_link + n, y_peer)
+        push(q, g, c_link + n, c_peer)
+
+    def z_arrivals(q, ns):
+        for n in ns:
+            z_arrival(q, n)
 
     def y_arrival(q, d):
-        g = slot(across(d), 1 - y, c)
+        g = slot(near(d), 1 - y, c)
         arrive(q, g)
         if q == spare and d == 0:
             push(q, g, spare_link, dev(across(1), y, c, x))
@@ -444,34 +456,41 @@
     mycol = pl.ds(pl.multiple_of(x * HD, HD), HD)
     itscol = pl.ds(pl.multiple_of((1 - x) * HD, HD), HD)
 
-    z_arrivals(0)
-    for q in range(chunks):
-        y_arrival(q, 0)
-    z_arrivals(1)
+    def finish(q):
+        for d in hops:
+            y_arrival(q, d)
+        c_arrivals(q)
+        partial(q)
+
+    q_msg = []
+
+    def finish_q(n):
+        finish(1 + n)
+        qm_s[n] = mix[1 + n, :, itscol].astype(bf)
+        q_msg.append(x_push(qm_s.at[n], qm_r.at[n]))
+
+    z_arrivals(0, hops)
+    y_arrival(0, 0)
+    y_arrival(1, 0)
+    own_z(chunks - 1)
+    y_arrival(2, 0)
+    z_arrivals(1, hops)
     for n, e in enumerate(plane):
         g = slot(*plane_dev(e))
         rcopy(gbuf.at[:, gcol(g)], gbuf.at[:, gcol(g)], g_send.at[n], g_recv.at[g], x_peer).wait_recv()
     norm(here)
-    for d in hops:
-        y_arrival(0, d)
     inv_msg.wait_recv()
     for cp in hid_msg:
         cp.wait_recv()
     inv_all[there, :] = jnp.broadcast_to(inv_r[:1, :], (toks, toks)).T
     norm(there)
-    c_arrivals(0)
-    partial(0)
+    finish(0)
     kv_s[...] = mix[0].astype(bf)
     kv_msg = x_push(kv_s, kv_r)
-    z_arrivals(2)
-    q_msg = []
-    for n in range(half):
-        for d in hops:
-            y_arrival(1 + n, d)
-        c_arrivals(1 + n)
-        partial(1 + n)
-        qm_s[n] = mix[1 + n, :, itscol].astype(bf)
-        q_msg.append(x_push(qm_s.at[n], qm_r.at[n]))
+    z_arrivals(2, hops[:-1])
+    finish_q(0)
+    z_arrivals(2, hops[-1:])
+    finish_q(1)
 
     loaded(cos_ref, nxt + 3)
     loaded(sin_ref, nxt + 4)
@@ -531,7 +550,7 @@
                      dev(across(d), y, c, x))
 
     order = ([far] if far else []) + hops[:far - 1 if far else None] + [0]
-    turn = chunks - 1
+    turn = 1
 
     def terms(q, grads, cc):
         part = nn_dot(ntr[pl.ds(pl.multiple_of(cc * chips * rows, rows), chips * rows), :], grads)
@@ -544,13 +563,15 @@
         to_core(q, k).wait_recv()
         return tbuf[q, c * chips + k].astype(f32) + rs1[q, k].astype(f32)
 
-    def rs_start(q, grads):
+    def rs_terms(q, grads):
         terms(q, grads, 1 - c)
         for yy in (1 - y, y):
             for d in order:
                 to_core(q, across(d) * SIDE + yy).start()
         terms(q, grads, c)
-        for d in order:
+
+    def rs_sums(q, ds):
+        for d in ds:
             part = core_sum(q, across(d) * SIDE + 1 - y)
             if q == turn and d == 0:
                 to_side(q, 0, ybuf.at[q, 1]).wait_recv()
@@ -616,12 +637,11 @@
 
     def rs_head(n):
         gq_msg[n].wait_recv()
-        rs_start(1 + n, jnp.concatenate([gq[n, 0], gq[n, 1]], axis=1))
-
-    for n in range(half):
-        inner, grad_keys, grad_values = head(n, inner, grad_keys, grad_values)
-        if n < half - 1:
-            rs_head(n)
+        rs_terms(1 + n, jnp.concatenate([gq[n, 0], gq[n, 1]], axis=1))
+
+    inner, grad_keys, grad_values = head(0, inner, grad_keys, grad_values)
+    rs_head(0)
+    inner, grad_keys, grad_values = head(1, inner, grad_keys, grad_values)
     grad_keys = unrope(grad_keys)
     gkv_s[:, :HD] = grad_keys.astype(bf)
     gkv_s[:, HD:] = grad_values.astype(bf)
@@ -632,12 +652,17 @@
     for n in range(half):
         attn_ref[:, pl.ds(pl.multiple_of((x * half + n) * HD, HD), HD)] = at_s[n, here, :]
 
-    rs_head(half - 1)
+    rs_sums(1, [d for d in order if d == 1] + [d for d in order if d > 1])
+    rs_head(1)
+    rs_sums(1, [0])
+    rs_sums(2, order)
     gkv_msg.wait_recv()
     keys_sum = gkv_s[:, :HD].astype(f32) + gkv_r[:, :HD].astype(f32)
     values_sum = gkv_s[:, HD:].astype(f32) + gkv_r[:, HD:].astype(f32)
     gkv_all = jnp.concatenate([keys_sum, values_sum], axis=1).astype(bf)
-    rs_start(0, gkv_all)
+    rs_terms(0, gkv_all)
+    rs_middle(1)
+    rs_sums(0, order)
     in_msg.wait_recv()
     inner = inner + jnp.broadcast_to(in_r[:1, :], (HD, seq)).T[:, :1]
     inner = inner + jnp.sum(gkv_all.astype(f32) * mix[0], axis=1, keepdims=True)
@@ -657,7 +682,6 @@
     at_msg = x_push(at_s.at[:, there], at_r)
 
     queue = list(range(1, chunks)) + [0]
-    rs_middle(queue[0])
     for p in range(PIECES):
         for b in range(span):
             j = p * span + b
@@ -823,7 +847,7 @@
         nz = n_inter // (CORES * SIDE)
         fits = n_intra == 2 and n_inter % (CORES * SIDE) == 0 and nz > 1 and nz & (nz - 1) == 0
         fits = fits and qkv_weight.shape[0] == HD and hidden_in.shape[0] == 1
-        fits = fits and hidden_in.shape[1] == HD and n_inter % PIECES == 0
+        fits = fits and hidden_in.shape[1] == HD and n_inter % PIECES == 0 and HEADS == 4 and nz == 4
         if fits:
             return fused(n_inter, hidden_in, norm_gain, qkv_weight, attn_cotangent)
         return local(hidden_in, norm_gain, qkv_weight, attn_cotangent)

time: 70.5 us -> 69.5 us (0.986)
  Pallas kernels: 69.7 us -> 68.7 us
    pallas_call x1, Pallas kernels: 68.5 us -> 67.6 us  [fused(): pl.pallas_call(functools.partial(fused_kernel, n_inter), out_shape=(V((to...]
where the time goes in v3:
time: 69.5 us; the launch traced here: 69.4 us
  Pallas kernels  68.7 us (99%)
    pallas_call x1, Pallas kernels, fused(): pl.pallas_call(functools.partial(fused_kernel, n_inter), out_shape=(V((to...  67.6 us

profile of v3, /device:TPU:1, one launch (start us, length us, event | category | flops | bytes accessed | tf_op | source)
XLA Modules:
  0.0 69.4 jit_solution(9207031465403429033)
XLA Ops:
  0.6 67.6 %shard_map.93 = (bf16[128,512]{1,0:T(8,128)(2,1)S(1)}, bf16[128,4096]{1,0:T(8,128)(2,1)S(1)}, f32[128,768]{1,0:T(8,128)S(1)}, f32[1,128]{1,0:T(1,128)S(1)}) custom-call(bf16[128,4096]{1,0:T(8,128)(2,1)} %bitcast.6, bf16[1,128]{1,0:T(2,128)(2,1)} %bitcast.8, bf16[128,768]{1,0:T(8,128)(2,1)} %w_ref.1, bf16[128,512]{1,0:T(8,128)(2,1)} %bitcast.7, ...), custom_call_target="tpu_custom_call" | custom-call | tf_op jit(solution)/shard_map/pallas_call | solution.py:772
  68.2 1.2 %shard_map.94 = (bf16[128,512]{1,0:T(8,128)(2,1)}, bf16[128,4096]{1,0:T(8,128)(2,1)}, f32[128,768]{1,0:T(8,128)}, f32[1,128]{1,0:T(1,128)}) custom-call(bf16[128,512]{1,0:T(8,128)(2,1)S(1)} %get-tuple-element.12.refs_0_, bf16[128,4096]{1,0:T(8,128)(2,1)S(1)} %get-tuple-element.13.refs_1_, f32[128,768]{1,0:T(8,128)S(1)} %get-tuple-element.14.refs_2_, ...), custom_call_target="tpu_custom_call" | custom-call | tf_op jit(solution)/shard_map/pallas_call | solution.py:832

commit v4 on v3

--- a/solution.py
+++ b/solution.py
@@ -234,6 +234,12 @@
 SIDE = 2
 PIECES = 4
 CHUNK = 2 * HD
+SPLIT = 1
+LAG = 1
+Z_AHEAD = 3
+Y_AHEAD = 3
+RELAYED = (0, 1, 2)
+MERGED = (1, 2)
 
 
 def nt_dot(a, b):
@@ -359,14 +365,16 @@
     pl.semaphore_wait(barrier, len(peers))
 
     inner_z = jnp.logical_and(z > 0, z < nz - 1)
-    far = nz - 1 if nz > 2 else None
-    spare = chunks - 1
-
-    def ag(q, g, link, device):
-        return rcopy(wbuf.at[q, g], wbuf.at[q, g], ag_send.at[q, link], ag_recv.at[q, g], device)
-
-    def arrive(q, g):
-        ag(q, g, 0, x_peer).wait_recv()
+    far = nz - 1
+    steps = chunks * SPLIT
+    spare = steps - 1
+
+    def ag(t, g, link, device):
+        part = wbuf.at[t // SPLIT, g, pl.ds(t % SPLIT * (rows // SPLIT), rows // SPLIT)]
+        return rcopy(part, part, ag_send.at[t, link], ag_recv.at[t, g], device)
+
+    def arrive(t, g):
+        ag(t, g, 0, x_peer).wait_recv()
 
     def x_copy(k, src, dst):
         return rcopy(src, dst, x_send.at[k], x_recv.at[k], x_peer)
@@ -376,8 +384,8 @@
     spare_link = 2 * nz + chips
     sent = []
 
-    def push(q, g, link, device, cond=None):
-        cp = ag(q, g, link, device)
+    def push(t, g, link, device, cond=None):
+        cp = ag(t, g, link, device)
         sent.append((cp, cond))
         if cond is None:
             cp.start()
@@ -387,15 +395,21 @@
     for n, e in enumerate(plane):
         rcopy(gbuf.at[:, gcol(own)], gbuf.at[:, gcol(own)], g_send.at[n], g_recv.at[own],
               dev(*plane_dev(e), x)).start()
-    def own_z(q):
-        for d in ([far] if far else []) + hops[::-1][1 if far else 0 :]:
-            push(q, own, d, dev(across(d), y, c, x), inner_z if d == far and q else None)
-
-    for q in range(chunks):
-        if q < chunks - 1:
-            own_z(q)
-        push(q, own, y_link, y_peer)
-        push(q, own, c_link, c_peer)
+    def own_z(t):
+        if t < steps:
+            for d in hops[::-1]:
+                push(t, own, d, dev(across(d), y, c, x), inner_z if d == far and t // SPLIT in RELAYED else None)
+
+    def own_y(t):
+        if t < steps:
+            push(t, own, y_link, y_peer)
+            push(t, own, c_link, c_peer)
+
+    for t in range(max(Z_AHEAD, Y_AHEAD)):
+        if t < Z_AHEAD:
+            own_z(t)
+        if t < Y_AHEAD:
+            own_y(t)
     messages = []
 
     def x_push(src, dst):
@@ -413,30 +427,36 @@
             return across(n)
         return jnp.where(inner_z, across(nz + 1 - n), across(n))
 
-    def z_arrival(q, n):
-        g = slot(near(n), y, c)
-        arrive(q, g)
-        if n == far and q:
-            push(q, g, 0, dev(across(1), y, c, x), inner_z)
-        if q != spare or n != 1:
-            push(q, g, y_link + n, y_peer)
-        push(q, g, c_link + n, c_peer)
-
-    def z_arrivals(q, ns):
-        for n in ns:
-            z_arrival(q, n)
-
-    def y_arrival(q, d):
-        g = slot(near(d), 1 - y, c)
-        arrive(q, g)
-        if q == spare and d == 0:
-            push(q, g, spare_link, dev(across(1), y, c, x))
-        push(q, g, c_link + nz + d, c_peer)
+    def z_arrivals(t):
+        for n in hops:
+            g = slot(near(n), y, c)
+            arrive(t, g)
+            if n == far and t // SPLIT in RELAYED:
+                push(t, g, 0, dev(across(1), y, c, x), inner_z)
+            if t != spare or n != 1:
+                push(t, g, y_link + n, y_peer)
+            push(t, g, c_link + n, c_peer)
+        own_z(t + Z_AHEAD)
+        own_y(t + Y_AHEAD)
+
+    def y_own(t):
+        g = slot(z, 1 - y, c)
+        arrive(t, g)
+        if t == spare:
+            push(t, g, spare_link, dev(across(1), y, c, x))
+        push(t, g, c_link + nz, c_peer)
+
+    def y_arrivals(t):
+        for n in hops:
+            g = slot(near(n), 1 - y, c)
+            arrive(t, g)
+            push(t, g, c_link + nz + n, c_peer)
 
     def c_arrivals(q):
-        for d in range(nz):
-            for yy in (y, 1 - y):
-                arrive(q, slot(across(d), yy, 1 - c))
+        for t in range(q * SPLIT, (q + 1) * SPLIT):
+            for d in range(nz):
+                for yy in (y, 1 - y):
+                    arrive(t, slot(across(d), yy, 1 - c))
 
     def norm(which):
         scaled = inv_all[which, :1]
@@ -447,50 +467,47 @@
             ntr[p * lanes : (p + 1) * lanes, which] = value.T
 
     def partial(q):
-        out = jnp.zeros((seq, CHUNK), f32)
+        out = [jnp.zeros((toks, CHUNK), f32)] * 2
         for p in range(PIECES):
             w = wbuf[q, p * span : (p + 1) * span].reshape(lanes, CHUNK)
-            out = out + nn_dot(nbuf[p], w)
-        mix[q] = out
+            out = [o + nn_dot(nbuf[p, r * toks : (r + 1) * toks, :], w) for r, o in enumerate(out)]
+        for r, o in enumerate(out):
+            mix[q, r * toks : (r + 1) * toks, :] = o
 
     mycol = pl.ds(pl.multiple_of(x * HD, HD), HD)
     itscol = pl.ds(pl.multiple_of((1 - x) * HD, HD), HD)
 
-    def finish(q):
-        for d in hops:
-            y_arrival(q, d)
-        c_arrivals(q)
-        partial(q)
-
     q_msg = []
 
-    def finish_q(n):
-        finish(1 + n)
+    def send_q(n):
+        c_arrivals(1 + n)
+        partial(1 + n)
         qm_s[n] = mix[1 + n, :, itscol].astype(bf)
         q_msg.append(x_push(qm_s.at[n], qm_r.at[n]))
 
-    z_arrivals(0, hops)
-    y_arrival(0, 0)
-    y_arrival(1, 0)
-    own_z(chunks - 1)
-    y_arrival(2, 0)
-    z_arrivals(1, hops)
-    for n, e in enumerate(plane):
-        g = slot(*plane_dev(e))
-        rcopy(gbuf.at[:, gcol(g)], gbuf.at[:, gcol(g)], g_send.at[n], g_recv.at[g], x_peer).wait_recv()
-    norm(here)
-    inv_msg.wait_recv()
-    for cp in hid_msg:
-        cp.wait_recv()
-    inv_all[there, :] = jnp.broadcast_to(inv_r[:1, :], (toks, toks)).T
-    norm(there)
-    finish(0)
-    kv_s[...] = mix[0].astype(bf)
-    kv_msg = x_push(kv_s, kv_r)
-    z_arrivals(2, hops[:-1])
-    finish_q(0)
-    z_arrivals(2, hops[-1:])
-    finish_q(1)
+    for t in range(steps + LAG):
+        if t < steps:
+            z_arrivals(t)
+            y_own(t)
+        if t == LAG:
+            for n, e in enumerate(plane):
+                g = slot(*plane_dev(e))
+                rcopy(gbuf.at[:, gcol(g)], gbuf.at[:, gcol(g)], g_send.at[n], g_recv.at[g], x_peer).wait_recv()
+            norm(here)
+        if t >= LAG:
+            y_arrivals(t - LAG)
+            if t - LAG == SPLIT - 1:
+                inv_msg.wait_recv()
+                for cp in hid_msg:
+                    cp.wait_recv()
+                inv_all[there, :] = jnp.broadcast_to(inv_r[:1, :], (toks, toks)).T
+                norm(there)
+                c_arrivals(0)
+                partial(0)
+                kv_s[...] = mix[0].astype(bf)
+                kv_msg = x_push(kv_s, kv_r)
+            if t - LAG == 2 * SPLIT - 1:
+                send_q(0)
 
     loaded(cos_ref, nxt + 3)
     loaded(sin_ref, nxt + 4)
@@ -549,15 +566,15 @@
         return rcopy(zbuf.at[q, d - 1], rs3.at[q, d - 1], z_send.at[q, d - 1], z_recv.at[q, d - 1],
                      dev(across(d), y, c, x))
 
-    order = ([far] if far else []) + hops[:far - 1 if far else None] + [0]
+    order = [far, 1, 2, 0]
     turn = 1
 
     def terms(q, grads, cc):
         part = nn_dot(ntr[pl.ds(pl.multiple_of(cc * chips * rows, rows), chips * rows), :], grads)
         tbuf[q, pl.ds(cc * chips, chips)] = part.astype(bf).reshape(chips, rows, CHUNK)
 
-    def to_side(q, k, src):
-        return rcopy(src, side.at[k, q], s_send.at[k, q], s_recv.at[k, q], dev(across(1), y, c, x))
+    def to_side(k, src):
+        return rcopy(src, side.at[k], s_send.at[k], s_recv.at[k], dev(across(1), y, c, x))
 
     def core_sum(q, k):
         to_core(q, k).wait_recv()
@@ -574,29 +591,29 @@
         for d in ds:
             part = core_sum(q, across(d) * SIDE + 1 - y)
             if q == turn and d == 0:
-                to_side(q, 0, ybuf.at[q, 1]).wait_recv()
-                part = part + side[0, q].astype(f32)
+                to_side(0, ybuf.at[q, 1]).wait_recv()
+                part = part + side[0].astype(f32)
             ybuf[q, d] = part.astype(bf)
             if q == turn and d == 1:
-                to_side(q, 0, ybuf.at[q, d]).start()
+                to_side(0, ybuf.at[q, d]).start()
             else:
                 to_y(q, d).start()
 
-    def rs_middle(q):
-        for d in order:
+    def rs_middle(q, ds):
+        for d in ds:
             part = core_sum(q, across(d) * SIDE + y)
             if q != turn or d != 1:
                 to_y(q, d).wait_recv()
                 part = part + rs2[q, d].astype(f32)
             if d == 0:
                 mix[q, :rows, :] = part
-            elif d == far:
+            elif d == far and q in MERGED:
                 zbuf[q, d - 1] = part.astype(bf)
                 pl.when(inner_z)(to_z(q, d).start)
-                pl.when(jnp.logical_not(inner_z))(to_side(q, 1, zbuf.at[q, d - 1]).start)
-            elif d == 2:
-                pl.when(inner_z)(to_side(q, 1, zbuf.at[q, d - 1]).wait_recv)
-                extra = jnp.where(inner_z, side[1, q].astype(f32), 0.0)
+                pl.when(jnp.logical_not(inner_z))(to_side(q, zbuf.at[q, d - 1]).start)
+            elif d == 2 and q in MERGED:
+                pl.when(inner_z)(to_side(q, zbuf.at[q, d - 1]).wait_recv)
+                extra = jnp.where(inner_z, side[q].astype(f32), 0.0)
                 zbuf[q, d - 1] = (part + extra).astype(bf)
                 to_z(q, d).start()
             else:
@@ -610,7 +627,7 @@
     def rs_end(q):
         result = mix[q, :rows, :]
         for d in hops:
-            if d == far:
+            if d == far and q in MERGED:
                 pl.when(inner_z)(to_z(q, d).wait_recv)
                 result = result + jnp.where(inner_z, rs3[q, d - 1].astype(f32), 0.0)
             else:
@@ -640,6 +657,7 @@
         rs_terms(1 + n, jnp.concatenate([gq[n, 0], gq[n, 1]], axis=1))
 
     inner, grad_keys, grad_values = head(0, inner, grad_keys, grad_values)
+    send_q(1)
     rs_head(0)
     inner, grad_keys, grad_values = head(1, inner, grad_keys, grad_values)
     grad_keys = unrope(grad_keys)
@@ -649,6 +667,7 @@
     inner_all = jnp.broadcast_to(inner, (seq, HD))
     in_s[...] = inner_all.T[:8, :]
     in_msg = x_push(in_s, in_r)
+    at_msg = x_push(at_s.at[:, there], at_r)
     for n in range(half):
         attn_ref[:, pl.ds(pl.multiple_of((x * half + n) * HD, HD), HD)] = at_s[n, here, :]
 
@@ -661,8 +680,7 @@
     values_sum = gkv_s[:, HD:].astype(f32) + gkv_r[:, HD:].astype(f32)
     gkv_all = jnp.concatenate([keys_sum, values_sum], axis=1).astype(bf)
     rs_terms(0, gkv_all)
-    rs_middle(1)
-    rs_sums(0, order)
+    rs_middle(1, [far, 1])
     in_msg.wait_recv()
     inner = inner + jnp.broadcast_to(in_r[:1, :], (HD, seq)).T[:, :1]
     inner = inner + jnp.sum(gkv_all.astype(f32) * mix[0], axis=1, keepdims=True)
@@ -679,25 +697,19 @@
         gain = gbuf[:, p * lanes : (p + 1) * lanes]
         gi_s[p] = (gain * out * inv[:, :1] - hx[p].astype(f32) * inv_all[:, :1]).astype(bf)
         gi_msg.append(x_push(gi_s.at[p, there], gi_r.at[p]))
-    at_msg = x_push(at_s.at[:, there], at_r)
-
     queue = list(range(1, chunks)) + [0]
+    rs_middle(1, [2])
+    rs_sums(0, order)
+    rs_middle(1, [0])
+    rs_middle(2, [far, 1])
     for p in range(PIECES):
         for b in range(span):
             j = p * span + b
             gin_ref[:, pl.ds(pl.multiple_of((2 * j + x) * rows, rows), rows)] = gi_s[p, here, b * rows : (b + 1) * rows]
-    for n in range(1, chunks):
-        rs_middle(queue[n])
-        rs_end(queue[n - 1])
-    rs_end(queue[-1])
-    lanes_sum = sums[0]
-    for part in sums[1:]:
-        lanes_sum = lanes_sum + part
-    gg = jnp.sum(lanes_sum.T, axis=0, keepdims=True) / gbuf[:, gcol(block)]
-    gg_ref[...] = gg
-    gg_s[...] = gg
-    pl.when(cross)(lambda: gg_copy.start())
-
+    rs_middle(2, [2, 0])
+    rs_end(1)
+    rs_middle(0, order)
+    rs_end(2)
     at_msg.wait_recv()
     for n in range(half):
         attn_ref[:, pl.ds(pl.multiple_of(((1 - x) * half + n) * HD, HD), HD)] = at_r[n]
@@ -706,6 +718,15 @@
         for b in range(span):
             j = p * span + b
             gin_ref[:, pl.ds(pl.multiple_of((2 * j + 1 - x) * rows, rows), rows)] = gi_r[p, :, b * rows : (b + 1) * rows]
+
+    rs_end(0)
+    lanes_sum = sums[0]
+    for part in sums[1:]:
+        lanes_sum = lanes_sum + part
+    gg = jnp.sum(lanes_sum.T, axis=0, keepdims=True) / gbuf[:, gcol(block)]
+    gg_ref[...] = gg
+    gg_s[...] = gg
+    pl.when(cross)(lambda: gg_copy.start())
 
     for cp, cond in sent:
         if cond is None:
@@ -723,11 +744,11 @@
             if q != turn or d != 1:
                 to_y(q, d).wait_send()
             else:
-                to_side(q, 0, ybuf.at[q, d]).wait_send()
+                to_side(0, ybuf.at[q, d]).wait_send()
         for d in hops:
-            if d == far:
+            if d == far and q in MERGED:
                 pl.when(inner_z)(to_z(q, d).wait_send)
-                pl.when(jnp.logical_not(inner_z))(to_side(q, 1, zbuf.at[q, d - 1]).wait_send)
+                pl.when(jnp.logical_not(inner_z))(to_side(q, zbuf.at[q, d - 1]).wait_send)
             else:
                 to_z(q, d).wait_send()
 
@@ -809,19 +830,19 @@
             V((chunks, nz, rows, CHUNK), bf),
             V((chunks, nz - 1, rows, CHUNK), bf),
             V((chunks, nz - 1, rows, CHUNK), bf),
-            V((2, chunks, rows, CHUNK), bf),
+            V((chunks, rows, CHUNK), bf),
             V((chunks, rows, CHUNK), bf),
             V((chunks, rows, CHUNK), bf),
             V((1, rows), f32),
             V((1, rows), f32),
             dma((8 + half,)),
-            dma((chunks, 2 * nz + chips + 1)), dma((chunks, n_inter)),
+            dma((chunks * SPLIT, 2 * nz + chips + 1)), dma((chunks * SPLIT, n_inter)),
             dma((n_inter,)), dma((n_inter,)),
             dma((n_msgs,)), dma((n_msgs,)),
             dma((chunks, chips)), dma((chunks, chips)),
             dma((chunks, nz)), dma((chunks, nz)),
             dma((chunks, nz - 1)), dma((chunks, nz - 1)),
-            dma((2, chunks)), dma((2, chunks)),
+            dma((chunks,)), dma((chunks,)),
             dma((chunks + 1,)), dma((chunks + 1,)),
         ],
         compiler_params=pltpu.CompilerParams(

time: 69.5 us -> 67.3 us (0.968)
  Pallas kernels: 68.7 us -> 66.5 us
    pallas_call x1, Pallas kernels: 67.6 us -> 65.3 us  [fused(): pl.pallas_call(functools.partial(fused_kernel, n_inter), out_shape=(V((to...]
where the time goes in v4:
time: 67.3 us; the launch traced here: 67.1 us
  Pallas kernels  66.5 us (99%)
    pallas_call x1, Pallas kernels, fused(): pl.pallas_call(functools.partial(fused_kernel, n_inter), out_shape=(V((to...  65.3 us

profile of v4, /device:TPU:1, one launch (start us, length us, event | category | flops | bytes accessed | tf_op | source)
XLA Modules:
  0.0 67.1 jit_solution(7308371507305124456)
XLA Ops:
  0.6 65.3 %shard_map.93 = (bf16[128,512]{1,0:T(8,128)(2,1)S(1)}, bf16[128,4096]{1,0:T(8,128)(2,1)S(1)}, f32[128,768]{1,0:T(8,128)S(1)}, f32[1,128]{1,0:T(1,128)S(1)}) custom-call(bf16[128,4096]{1,0:T(8,128)(2,1)} %bitcast.6, bf16[1,128]{1,0:T(2,128)(2,1)} %bitcast.8, bf16[128,768]{1,0:T(8,128)(2,1)} %w_ref.1, bf16[128,512]{1,0:T(8,128)(2,1)} %bitcast.7, ...), custom_call_target="tpu_custom_call" | custom-call | tf_op jit(solution)/shard_map/pallas_call | solution.py:793
  66.0 1.2 %shard_map.94 = (bf16[128,512]{1,0:T(8,128)(2,1)}, bf16[128,4096]{1,0:T(8,128)(2,1)}, f32[128,768]{1,0:T(8,128)}, f32[1,128]{1,0:T(1,128)}) custom-call(bf16[128,512]{1,0:T(8,128)(2,1)S(1)} %get-tuple-element.12.refs_0_, bf16[128,4096]{1,0:T(8,128)(2,1)S(1)} %get-tuple-element.13.refs_1_, f32[128,768]{1,0:T(8,128)S(1)} %get-tuple-element.14.refs_2_, ...), custom_call_target="tpu_custom_call" | custom-call | tf_op jit(solution)/shard_map/pallas_call | solution.py:853

commit v5 on v4

--- a/solution.py
+++ b/solution.py
@@ -236,9 +236,8 @@
 CHUNK = 2 * HD
 SPLIT = 1
 LAG = 1
-Z_AHEAD = 3
-Y_AHEAD = 3
-RELAYED = (0, 1, 2)
+HELD = 2
+HELD_UNTIL = 0
 MERGED = (1, 2)
 
 
@@ -261,8 +260,8 @@
     wbuf, gbuf, gain_in, hx, hs, nbuf, ntr, inv_all, inv_s, inv_r, ctb, cts, cos_ref, sin_ref,
     mix, kv_s, kv_r, qm_s, qm_r, gq, gkv_s, gkv_r, in_s, in_r, at_s, at_r, gi_s, gi_r,
     tbuf, rs1, ybuf, rs2, zbuf, rs3, side, dg_s, dg_r, gg_s, gg_r,
-    ld_sem, ag_send, ag_recv, g_send, g_recv, x_send, x_recv,
-    c_send, c_recv, y_send, y_recv, z_send, z_recv, s_send, s_recv, d_send, d_recv,
+    ld_sem, ag_send, ag_recv, ag_core, g_sem, x_send, x_recv,
+    c_send, c_recv, r_send, y_recv, z_recv, s_recv, d_send, d_recv,
 ):
     i = lax.axis_index("inter")
     x = lax.axis_index("intra")
@@ -338,8 +337,8 @@
     for n in range(half):
         for xx in range(2):
             first = (xx * half + n) * HD
-            load(w_ref.at[:, first : first + HD], wbuf.at[1 + n, own, :, xx * HD : (xx + 1) * HD], 3 + n)
-    nxt = 3 + half
+            load(w_ref.at[:, first : first + HD], wbuf.at[1 + n, own, :, xx * HD : (xx + 1) * HD], 2)
+    nxt = 3
     load(gain_ref, gain_in, nxt)
     load(ct_ref.at[:, pl.ds(pl.multiple_of(x * half * HD, HD), half * HD)], ctb.at[here], nxt + 1)
     load(ct_ref.at[:, pl.ds(pl.multiple_of((1 - x) * half * HD, HD), half * HD)], cts, nxt + 2)
@@ -359,8 +358,7 @@
     inv = jnp.broadcast_to(lax.rsqrt(total / width + eps_norm), (toks, HD))
     inv_all[here, :] = inv
     inv_s[...] = inv.T[:8, :]
-    for q in range(chunks):
-        loaded(wbuf.at[q, own], 2 + q)
+    loaded(wbuf.at[:, own], 2)
     loaded(cts, nxt + 2)
     pl.semaphore_wait(barrier, len(peers))
 
@@ -369,57 +367,61 @@
     steps = chunks * SPLIT
     spare = steps - 1
 
-    def ag(t, g, link, device):
+    def ag(t, g, device, core=False):
         part = wbuf.at[t // SPLIT, g, pl.ds(t % SPLIT * (rows // SPLIT), rows // SPLIT)]
-        return rcopy(part, part, ag_send.at[t, link], ag_recv.at[t, g], device)
+        rs = ag_core.at[t] if core else ag_recv.at[t, g // CORES]
+        return rcopy(part, part, ag_send.at[t], rs, device)
 
     def arrive(t, g):
-        ag(t, g, 0, x_peer).wait_recv()
-
-    def x_copy(k, src, dst):
-        return rcopy(src, dst, x_send.at[k], x_recv.at[k], x_peer)
-
-    y_link = nz
-    c_link = 2 * nz
-    spare_link = 2 * nz + chips
-    sent = []
-
-    def push(t, g, link, device, cond=None):
-        cp = ag(t, g, link, device)
-        sent.append((cp, cond))
+        ag(t, g, x_peer).wait_recv()
+
+    def sent_all(ref, sem):
+        rcopy(ref, ref, sem, d_recv.at[0], x_peer).wait_send()
+
+    def got_all(ref, sem):
+        rcopy(ref, ref, d_send.at[0], sem, x_peer).wait_recv()
+
+    def push(t, g, device, core=False, cond=None):
+        cp = ag(t, g, device, core)
         if cond is None:
             cp.start()
         else:
             pl.when(cond)(cp.start)
 
     for n, e in enumerate(plane):
-        rcopy(gbuf.at[:, gcol(own)], gbuf.at[:, gcol(own)], g_send.at[n], g_recv.at[own],
+        rcopy(gbuf.at[:, gcol(own)], gbuf.at[:, gcol(own)], g_sem.at[0], g_sem.at[1],
               dev(*plane_dev(e), x)).start()
-    def own_z(t):
-        if t < steps:
-            for d in hops[::-1]:
-                push(t, own, d, dev(across(d), y, c, x), inner_z if d == far and t // SPLIT in RELAYED else None)
+    ends_z = jnp.logical_not(inner_z)
+
+    def own_z(t, late=False):
+        for d in hops[::-1]:
+            if d == far:
+                cond = inner_z
+            else:
+                cond = (inner_z if late else ends_z) if t >= HELD else None
+            if d != far or not late:
+                push(t, own, dev(across(d), y, c, x), cond=cond)
 
     def own_y(t):
-        if t < steps:
-            push(t, own, y_link, y_peer)
-            push(t, own, c_link, c_peer)
-
-    for t in range(max(Z_AHEAD, Y_AHEAD)):
-        if t < Z_AHEAD:
-            own_z(t)
-        if t < Y_AHEAD:
-            own_y(t)
+        push(t, own, y_peer)
+        push(t, own, c_peer, core=True)
+
+    for t in range(steps):
+        own_z(t)
+        own_y(t)
     messages = []
 
-    def x_push(src, dst):
-        cp = x_copy(len(messages), src, dst)
+    def x_push(src, dst, ss=0, rs=None):
+        if rs is None:
+            rs = len(messages) + 2
+            messages.append(rs)
+        cp = rcopy(src, dst, x_send.at[ss], x_recv.at[rs], x_peer)
         cp.start()
-        messages.append(cp)
         return cp
 
-    inv_msg = x_push(inv_s, inv_r)
-    hid_msg = [x_push(hs.at[p], hx.at[p, here]) for p in range(PIECES)]
+    inv_msg = x_push(inv_s, inv_r, 1)
+    for p in range(PIECES):
+        x_push(hs.at[p], hx.at[p, here], 0, 0)
     ct_msg = x_push(cts, ctb.at[here])
 
     def near(n):
@@ -431,32 +433,31 @@
         for n in hops:
             g = slot(near(n), y, c)
             arrive(t, g)
-            if n == far and t // SPLIT in RELAYED:
-                push(t, g, 0, dev(across(1), y, c, x), inner_z)
+            if n == far:
+                push(t, g, dev(across(1), y, c, x), cond=inner_z)
             if t != spare or n != 1:
-                push(t, g, y_link + n, y_peer)
-            push(t, g, c_link + n, c_peer)
-        own_z(t + Z_AHEAD)
-        own_y(t + Y_AHEAD)
+                push(t, g, y_peer)
+            push(t, g, c_peer, core=True)
+        if t == HELD_UNTIL:
+            for k in range(HELD, steps):
+                own_z(k, True)
 
     def y_own(t):
         g = slot(z, 1 - y, c)
         arrive(t, g)
         if t == spare:
-            push(t, g, spare_link, dev(across(1), y, c, x))
-        push(t, g, c_link + nz, c_peer)
+            push(t, g, dev(across(1), y, c, x))
+        push(t, g, c_peer, core=True)
 
     def y_arrivals(t):
         for n in hops:
             g = slot(near(n), 1 - y, c)
             arrive(t, g)
-            push(t, g, c_link + nz + n, c_peer)
+            push(t, g, c_peer, core=True)
 
     def c_arrivals(q):
         for t in range(q * SPLIT, (q + 1) * SPLIT):
-            for d in range(nz):
-                for yy in (y, 1 - y):
-                    arrive(t, slot(across(d), yy, 1 - c))
+            got_all(wbuf.at[q, :chips, pl.ds(t % SPLIT * (rows // SPLIT), rows // SPLIT)], ag_core.at[t])
 
     def norm(which):
         scaled = inv_all[which, :1]
@@ -490,16 +491,13 @@
             z_arrivals(t)
             y_own(t)
         if t == LAG:
-            for n, e in enumerate(plane):
-                g = slot(*plane_dev(e))
-                rcopy(gbuf.at[:, gcol(g)], gbuf.at[:, gcol(g)], g_send.at[n], g_recv.at[g], x_peer).wait_recv()
+            got_all(gbuf.at[:, : len(plane) * rows], g_sem.at[1])
             norm(here)
         if t >= LAG:
             y_arrivals(t - LAG)
             if t - LAG == SPLIT - 1:
                 inv_msg.wait_recv()
-                for cp in hid_msg:
-                    cp.wait_recv()
+                got_all(hs, x_recv.at[0])
                 inv_all[there, :] = jnp.broadcast_to(inv_r[:1, :], (toks, toks)).T
                 norm(there)
                 c_arrivals(0)
@@ -557,13 +555,13 @@
         return inner, grad_keys, grad_values
 
     def to_core(q, k):
-        return rcopy(tbuf.at[q, (1 - c) * chips + k], rs1.at[q, k], c_send.at[q, k], c_recv.at[q, k], c_peer)
+        return rcopy(tbuf.at[q, (1 - c) * chips + k], rs1.at[q, k], c_send, c_recv.at[q, lax.rem(k + y, 2)], c_peer)
 
     def to_y(q, d):
-        return rcopy(ybuf.at[q, d], rs2.at[q, d], y_send.at[q, d], y_recv.at[q, d], y_peer)
+        return rcopy(ybuf.at[q, d], rs2.at[q, d], r_send, y_recv.at[q, d], y_peer)
 
     def to_z(q, d):
-        return rcopy(zbuf.at[q, d - 1], rs3.at[q, d - 1], z_send.at[q, d - 1], z_recv.at[q, d - 1],
+        return rcopy(zbuf.at[q, d - 1], rs3.at[q, d - 1], r_send, z_recv.at[q],
                      dev(across(d), y, c, x))
 
     order = [far, 1, 2, 0]
@@ -574,10 +572,9 @@
         tbuf[q, pl.ds(cc * chips, chips)] = part.astype(bf).reshape(chips, rows, CHUNK)
 
     def to_side(k, src):
-        return rcopy(src, side.at[k], s_send.at[k], s_recv.at[k], dev(across(1), y, c, x))
+        return rcopy(src, side.at[k], r_send, s_recv.at[k], dev(across(1), y, c, x))
 
     def core_sum(q, k):
-        to_core(q, k).wait_recv()
         return tbuf[q, c * chips + k].astype(f32) + rs1[q, k].astype(f32)
 
     def rs_terms(q, grads):
@@ -588,6 +585,8 @@
         terms(q, grads, c)
 
     def rs_sums(q, ds):
+        if ds[0]:
+            got_all(rs1.at[q, :nz], c_recv.at[q, 1])
         for d in ds:
             part = core_sum(q, across(d) * SIDE + 1 - y)
             if q == turn and d == 0:
@@ -600,6 +599,8 @@
                 to_y(q, d).start()
 
     def rs_middle(q, ds):
+        if ds[0] == far:
+            got_all(rs1.at[q, :nz], c_recv.at[q, 0])
         for d in ds:
             part = core_sum(q, across(d) * SIDE + y)
             if q != turn or d != 1:
@@ -626,13 +627,14 @@
 
     def rs_end(q):
         result = mix[q, :rows, :]
+        if q in MERGED:
+            pl.when(inner_z)(lambda: got_all(rs3.at[q], z_recv.at[q]))
+            pl.when(ends_z)(lambda: got_all(rs3.at[q, : far - 1], z_recv.at[q]))
+        else:
+            got_all(rs3.at[q], z_recv.at[q])
         for d in hops:
-            if d == far and q in MERGED:
-                pl.when(inner_z)(to_z(q, d).wait_recv)
-                result = result + jnp.where(inner_z, rs3[q, d - 1].astype(f32), 0.0)
-            else:
-                to_z(q, d).wait_recv()
-                result = result + rs3[q, d - 1].astype(f32)
+            part = rs3[q, d - 1].astype(f32)
+            result = result + (jnp.where(inner_z, part, 0.0) if d == far and q in MERGED else part)
         prod = wbuf[q, block].astype(f32) * result
         sums.append(prod[:, :HD] + prod[:, HD:])
         dg_s[q] = result.astype(bf)
@@ -648,9 +650,9 @@
                 wg_ref[:, first : first + HD] = result[:, xx * HD : (xx + 1) * HD]
 
     def to_diag(q):
-        return rcopy(dg_s.at[q], dg_r.at[q], d_send.at[q], d_recv.at[q], d_peer)
-
-    gg_copy = rcopy(gg_s, gg_r, d_send.at[chunks], d_recv.at[chunks], d_peer)
+        return rcopy(dg_s.at[q], dg_r.at[q], d_send.at[0], d_recv.at[0], d_peer)
+
+    gg_copy = rcopy(gg_s, gg_r, d_send.at[1], d_recv.at[1], d_peer)
 
     def rs_head(n):
         gq_msg[n].wait_recv()
@@ -666,7 +668,7 @@
     gkv_msg = x_push(gkv_s, gkv_r)
     inner_all = jnp.broadcast_to(inner, (seq, HD))
     in_s[...] = inner_all.T[:8, :]
-    in_msg = x_push(in_s, in_r)
+    in_msg = x_push(in_s, in_r, 2)
     at_msg = x_push(at_s.at[:, there], at_r)
     for n in range(half):
         attn_ref[:, pl.ds(pl.multiple_of((x * half + n) * HD, HD), HD)] = at_s[n, here, :]
@@ -688,7 +690,6 @@
     inv_all[...] = inner * (inv * inv / width)
 
     gqs = [jnp.concatenate([gq[n, 0], gq[n, 1]], axis=1) for n in range(half)]
-    gi_msg = []
     for p in range(PIECES):
         out = jnp.zeros((seq, lanes), f32)
         for q in range(chunks):
@@ -696,7 +697,7 @@
             out = out + nt_dot(gkv_all if q == 0 else gqs[q - 1], w)
         gain = gbuf[:, p * lanes : (p + 1) * lanes]
         gi_s[p] = (gain * out * inv[:, :1] - hx[p].astype(f32) * inv_all[:, :1]).astype(bf)
-        gi_msg.append(x_push(gi_s.at[p, there], gi_r.at[p]))
+        x_push(gi_s.at[p, there], gi_r.at[p], 0, 1)
     queue = list(range(1, chunks)) + [0]
     rs_middle(1, [2])
     rs_sums(0, order)
@@ -713,8 +714,8 @@
     at_msg.wait_recv()
     for n in range(half):
         attn_ref[:, pl.ds(pl.multiple_of(((1 - x) * half + n) * HD, HD), HD)] = at_r[n]
+    got_all(gi_r, x_recv.at[1])
     for p in range(PIECES):
-        gi_msg[p].wait_recv()
         for b in range(span):
             j = p * span + b
             gin_ref[:, pl.ds(pl.multiple_of((2 * j + 1 - x) * rows, rows), rows)] = gi_r[p, :, b * rows : (b + 1) * rows]
@@ -728,39 +729,26 @@
     gg_s[...] = gg
     pl.when(cross)(lambda: gg_copy.start())
 
-    for cp, cond in sent:
-        if cond is None:
-            cp.wait_send()
-        else:
-            pl.when(cond)(cp.wait_send)
-    for cp in messages:
-        cp.wait_send()
-    for n, e in enumerate(plane):
-        rcopy(gbuf.at[:, gcol(own)], gbuf.at[:, gcol(own)], g_send.at[n], g_recv.at[own], x_peer).wait_send()
-    for q in range(chunks):
-        for k in range(chips):
-            to_core(q, k).wait_send()
-        for d in range(nz):
-            if q != turn or d != 1:
-                to_y(q, d).wait_send()
-            else:
-                to_side(0, ybuf.at[q, d]).wait_send()
-        for d in hops:
-            if d == far and q in MERGED:
-                pl.when(inner_z)(to_z(q, d).wait_send)
-                pl.when(jnp.logical_not(inner_z))(to_side(q, zbuf.at[q, d - 1]).wait_send)
-            else:
-                to_z(q, d).wait_send()
+    for t in range(steps):
+        near_sends = wbuf.at[t // SPLIT, : n_inter - 2, pl.ds(0, rows // SPLIT)]
+        all_sends = wbuf.at[t // SPLIT, :, pl.ds(0, rows // SPLIT)]
+        pl.when(inner_z)(lambda: sent_all(all_sends, ag_send.at[t]))
+        pl.when(ends_z)(lambda: sent_all(near_sends, ag_send.at[t]))
+    sent_all(gbuf.at[:, : len(plane) * rows], g_sem.at[0])
+    sent_all(wbuf.at[:2, :13], x_send.at[0])
+    sent_all(inv_s, x_send.at[1])
+    sent_all(in_s, x_send.at[2])
+    sent_all(tbuf.at[:, :chips], c_send)
+    sent_all(tbuf.at[:, :7], r_send)
 
     @pl.when(cross)
     def _():
-        for q in queue:
-            to_diag(q).wait_recv()
+        got_all(dg_r, d_recv.at[0])
+        for q in range(chunks):
             store(q, dg_r[q].astype(f32))
         gg_copy.wait_recv()
         gg_ref[...] = gg_r[...]
-        for q in range(chunks):
-            to_diag(q).wait_send()
+        sent_all(dg_s, d_send.at[0])
         gg_copy.wait_send()
 
 
@@ -788,7 +776,6 @@
     vmem = pl.BlockSpec(memory_space=pltpu.VMEM)
     hbm = pl.BlockSpec(memory_space=pltpu.HBM)
     V = pltpu.VMEM
-    n_msgs = 2 * PIECES + 2 * half + 6
     ins = (hidden_in[0], norm_gain[None], qkv_weight, attn_cotangent[0], jnp.asarray(cosine), jnp.asarray(sine))
     attn, gin, wg, gg = pl.pallas_call(
         functools.partial(fused_kernel, n_inter),
@@ -835,15 +822,11 @@
             V((chunks, rows, CHUNK), bf),
             V((1, rows), f32),
             V((1, rows), f32),
-            dma((8 + half,)),
-            dma((chunks * SPLIT, 2 * nz + chips + 1)), dma((chunks * SPLIT, n_inter)),
-            dma((n_inter,)), dma((n_inter,)),
-            dma((n_msgs,)), dma((n_msgs,)),
-            dma((chunks, chips)), dma((chunks, chips)),
-            dma((chunks, nz)), dma((chunks, nz)),
-            dma((chunks, nz - 1)), dma((chunks, nz - 1)),
-            dma((chunks,)), dma((chunks,)),
-            dma((chunks + 1,)), dma((chunks + 1,)),
+            dma((8,)),
+            dma((chunks * SPLIT,)), dma((chunks * SPLIT, chips)), dma((chunks * SPLIT,)),
+            dma((2,)), dma((3,)), dma((12,)),
+            dma, dma((chunks, 2)), dma, dma((chunks, nz)), dma((chunks,)), dma((chunks,)),
+            dma((2,)), dma((2,)),
         ],
         compiler_params=pltpu.CompilerParams(
             collective_id=0, has_side_effects=True, vmem_limit_bytes=32 * 2**20

time: 67.3 us -> 65.6 us (0.975)
  Pallas kernels: 66.5 us -> 64.8 us
    pallas_call x1, Pallas kernels: 65.3 us -> 63.6 us  [fused(): pl.pallas_call(functools.partial(fused_kernel, n_inter), out_shape=(V((to...]
where the time goes in v5:
time: 65.6 us; the launch traced here: 65.4 us
  Pallas kernels  64.8 us (99%)
    pallas_call x1, Pallas kernels, fused(): pl.pallas_call(functools.partial(fused_kernel, n_inter), out_shape=(V((to...  63.6 us

profile of v5, /device:TPU:1, one launch (start us, length us, event | category | flops | bytes accessed | tf_op | source)
XLA Modules:
  0.0 65.4 jit_solution(14520250044172783554)
XLA Ops:
  0.6 63.6 %shard_map.93 = (bf16[128,512]{1,0:T(8,128)(2,1)S(1)}, bf16[128,4096]{1,0:T(8,128)(2,1)S(1)}, f32[128,768]{1,0:T(8,128)S(1)}, f32[1,128]{1,0:T(1,128)S(1)}) custom-call(bf16[128,4096]{1,0:T(8,128)(2,1)} %bitcast.6, bf16[1,128]{1,0:T(2,128)(2,1)} %bitcast.8, bf16[128,768]{1,0:T(8,128)(2,1)} %w_ref.1, bf16[128,512]{1,0:T(8,128)(2,1)} %bitcast.7, ...), custom_call_target="tpu_custom_call" | custom-call | tf_op jit(solution)/shard_map/pallas_call | solution.py:780
  64.2 1.2 %shard_map.94 = (bf16[128,512]{1,0:T(8,128)(2,1)}, bf16[128,4096]{1,0:T(8,128)(2,1)}, f32[128,768]{1,0:T(8,128)}, f32[1,128]{1,0:T(1,128)}) custom-call(bf16[128,512]{1,0:T(8,128)(2,1)S(1)} %get-tuple-element.12.refs_0_, bf16[128,4096]{1,0:T(8,128)(2,1)S(1)} %get-tuple-element.13.refs_1_, f32[128,768]{1,0:T(8,128)S(1)} %get-tuple-element.14.refs_2_, ...), custom_call_target="tpu_custom_call" | custom-call | tf_op jit(solution)/shard_map/pallas_call | solution.py:836

commit v6 on v5

--- a/solution.py
+++ b/solution.py
@@ -259,7 +259,7 @@
     attn_ref, gin_ref, wg_ref, gg_ref,
     wbuf, gbuf, gain_in, hx, hs, nbuf, ntr, inv_all, inv_s, inv_r, ctb, cts, cos_ref, sin_ref,
     mix, kv_s, kv_r, qm_s, qm_r, gq, gkv_s, gkv_r, in_s, in_r, at_s, at_r, gi_s, gi_r,
-    tbuf, rs1, ybuf, rs2, zbuf, rs3, side, dg_s, dg_r, gg_s, gg_r,
+    tbuf, rs1, ybuf, rs2, zbuf, rs3, side, dg_s, dg_r, gg_s, gg_r, w_own, gain_own,
     ld_sem, ag_send, ag_recv, ag_core, g_sem, x_send, x_recv,
     c_send, c_recv, r_send, y_recv, z_recv, s_recv, d_send, d_recv,
 ):
@@ -562,7 +562,7 @@
 
     def to_z(q, d):
         return rcopy(zbuf.at[q, d - 1], rs3.at[q, d - 1], r_send, z_recv.at[q],
-                     dev(across(d), y, c, x))
+                     dev(across(d), y, x, c) if q == 0 else dev(across(d), y, c, x))
 
     order = [far, 1, 2, 0]
     turn = 1
@@ -608,6 +608,9 @@
                 part = part + rs2[q, d].astype(f32)
             if d == 0:
                 mix[q, :rows, :] = part
+                if q == 0:
+                    dg_s[q] = part.astype(bf)
+                    pl.when(cross)(to_diag(q).start)
             elif d == far and q in MERGED:
                 zbuf[q, d - 1] = part.astype(bf)
                 pl.when(inner_z)(to_z(q, d).start)
@@ -621,12 +624,19 @@
                 zbuf[q, d - 1] = part.astype(bf)
                 to_z(q, d).start()
 
-    block = c * chips + z * SIDE + y
-    cross = c != x
     sums = []
+
+    def gain_term(parts, gain):
+        lanes_sum = parts[0]
+        for part in parts[1:]:
+            lanes_sum = lanes_sum + part
+        return jnp.sum(lanes_sum.T, axis=0, keepdims=True) / gain
 
     def rs_end(q):
         result = mix[q, :rows, :]
+        if q == 0:
+            pl.when(cross)(to_diag(q).wait_recv)
+            result = jnp.where(cross, dg_r[q].astype(f32), result)
         if q in MERGED:
             pl.when(inner_z)(lambda: got_all(rs3.at[q], z_recv.at[q]))
             pl.when(ends_z)(lambda: got_all(rs3.at[q, : far - 1], z_recv.at[q]))
@@ -635,11 +645,16 @@
         for d in hops:
             part = rs3[q, d - 1].astype(f32)
             result = result + (jnp.where(inner_z, part, 0.0) if d == far and q in MERGED else part)
-        prod = wbuf[q, block].astype(f32) * result
-        sums.append(prod[:, :HD] + prod[:, HD:])
-        dg_s[q] = result.astype(bf)
-        pl.when(cross)(lambda: to_diag(q).start())
         store(q, result)
+        if q:
+            prod = wbuf[q, block].astype(f32) * result
+            sums.append(prod[:, :HD] + prod[:, HD:])
+            dg_s[q] = result.astype(bf)
+            pl.when(cross)(to_diag(q).start)
+            return
+        prod = jnp.where(cross, w_own[...], wbuf[q, block]).astype(f32) * result
+        gain = jnp.where(cross, gain_own[...], gbuf[:, gcol(block)])
+        gg_ref[...] = gain_term([prod[:, :HD] + prod[:, HD:]], gain) + jnp.where(cross, gg_r[...], gg_s[...])
 
     def store(q, result):
         if q == 0:
@@ -648,11 +663,6 @@
             for xx in range(2):
                 first = (xx * half + q - 1) * HD
                 wg_ref[:, first : first + HD] = result[:, xx * HD : (xx + 1) * HD]
-
-    def to_diag(q):
-        return rcopy(dg_s.at[q], dg_r.at[q], d_send.at[0], d_recv.at[0], d_peer)
-
-    gg_copy = rcopy(gg_s, gg_r, d_send.at[1], d_recv.at[1], d_peer)
 
     def rs_head(n):
         gq_msg[n].wait_recv()
@@ -670,6 +680,17 @@
     in_s[...] = inner_all.T[:8, :]
     in_msg = x_push(in_s, in_r, 2)
     at_msg = x_push(at_s.at[:, there], at_r)
+    block = c * chips + z * SIDE + y
+    cross = c != x
+
+    def to_diag(q):
+        return rcopy(dg_s.at[q], dg_r.at[q], d_send.at[0], d_recv.at[min(q, 1)], d_peer)
+
+    w_copy = rcopy(wbuf.at[0, block], w_own, d_send.at[0], d_recv.at[2], d_peer)
+    gain_copy = rcopy(gbuf.at[:, gcol(block)], gain_own, d_send.at[1], d_recv.at[3], d_peer)
+    gg_copy = rcopy(gg_s, gg_r, d_send.at[1], d_recv.at[4], d_peer)
+    pl.when(cross)(w_copy.start)
+    pl.when(cross)(gain_copy.start)
     for n in range(half):
         attn_ref[:, pl.ds(pl.multiple_of((x * half + n) * HD, HD), HD)] = at_s[n, here, :]
 
@@ -711,6 +732,8 @@
     rs_end(1)
     rs_middle(0, order)
     rs_end(2)
+    gg_s[...] = gain_term(sums, gbuf[:, gcol(block)])
+    pl.when(cross)(gg_copy.start)
     at_msg.wait_recv()
     for n in range(half):
         attn_ref[:, pl.ds(pl.multiple_of(((1 - x) * half + n) * HD, HD), HD)] = at_r[n]
@@ -720,15 +743,17 @@
             j = p * span + b
             gin_ref[:, pl.ds(pl.multiple_of((2 * j + 1 - x) * rows, rows), rows)] = gi_r[p, :, b * rows : (b + 1) * rows]
 
+
+    @pl.when(cross)
+    def _():
+        w_copy.wait_recv()
+        gain_copy.wait_recv()
+        gg_copy.wait_recv()
+        got_all(dg_r.at[1:], d_recv.at[1])
+        for q in range(1, chunks):
+            store(q, dg_r[q].astype(f32))
+
     rs_end(0)
-    lanes_sum = sums[0]
-    for part in sums[1:]:
-        lanes_sum = lanes_sum + part
-    gg = jnp.sum(lanes_sum.T, axis=0, keepdims=True) / gbuf[:, gcol(block)]
-    gg_ref[...] = gg
-    gg_s[...] = gg
-    pl.when(cross)(lambda: gg_copy.start())
-
     for t in range(steps):
         near_sends = wbuf.at[t // SPLIT, : n_inter - 2, pl.ds(0, rows // SPLIT)]
         all_sends = wbuf.at[t // SPLIT, :, pl.ds(0, rows // SPLIT)]
@@ -743,13 +768,8 @@
 
     @pl.when(cross)
     def _():
-        got_all(dg_r, d_recv.at[0])
-        for q in range(chunks):
-            store(q, dg_r[q].astype(f32))
-        gg_copy.wait_recv()
-        gg_ref[...] = gg_r[...]
-        sent_all(dg_s, d_send.at[0])
-        gg_copy.wait_send()
+        sent_all(wbuf.at[0, : chunks + 1], d_send.at[0])
+        sent_all(gbuf.at[:, : 2 * rows], d_send.at[1])
 
 
 def copy_kernel(*refs):
@@ -822,11 +842,13 @@
             V((chunks, rows, CHUNK), bf),
             V((1, rows), f32),
             V((1, rows), f32),
+            V((rows, CHUNK), bf),
+            V((1, rows), f32),
             dma((8,)),
             dma((chunks * SPLIT,)), dma((chunks * SPLIT, chips)), dma((chunks * SPLIT,)),
             dma((2,)), dma((3,)), dma((12,)),
             dma, dma((chunks, 2)), dma, dma((chunks, nz)), dma((chunks,)), dma((chunks,)),
-            dma((2,)), dma((2,)),
+            dma((2,)), dma((5,)),
         ],
         compiler_params=pltpu.CompilerParams(
             collective_id=0, has_side_effects=True, vmem_limit_bytes=32 * 2**20

time: 65.6 us -> 63.9 us (0.974)
  Pallas kernels: 64.8 us -> 63 us
    pallas_call x1, Pallas kernels: 63.6 us -> 61.8 us  [fused(): pl.pallas_call(functools.partial(fused_kernel, n_inter), out_shape=(V((to...]
where the time goes in v6:
time: 63.9 us; the launch traced here: 63.7 us
  Pallas kernels  63 us (99%)
  between operations  0.64 us (1%)
    pallas_call x1, Pallas kernels, fused(): pl.pallas_call(functools.partial(fused_kernel, n_inter), out_shape=(V((to...  61.8 us

profile of v6, /device:TPU:1, one launch (start us, length us, event | category | flops | bytes accessed | tf_op | source)
XLA Modules:
  0.0 63.7 jit_solution(9515038065675407977)
XLA Ops:
  0.6 61.8 %shard_map.93 = (bf16[128,512]{1,0:T(8,128)(2,1)S(1)}, bf16[128,4096]{1,0:T(8,128)(2,1)S(1)}, f32[128,768]{1,0:T(8,128)S(1)}, f32[1,128]{1,0:T(1,128)S(1)}) custom-call(bf16[128,4096]{1,0:T(8,128)(2,1)} %bitcast.6, bf16[1,128]{1,0:T(2,128)(2,1)} %bitcast.8, bf16[128,768]{1,0:T(8,128)(2,1)} %w_ref.1, bf16[128,512]{1,0:T(8,128)(2,1)} %bitcast.7, ...), custom_call_target="tpu_custom_call" | custom-call | tf_op jit(solution)/shard_map/pallas_call | solution.py:800
  62.5 1.2 %shard_map.94 = (bf16[128,512]{1,0:T(8,128)(2,1)}, bf16[128,4096]{1,0:T(8,128)(2,1)}, f32[128,768]{1,0:T(8,128)}, f32[1,128]{1,0:T(1,128)}) custom-call(bf16[128,512]{1,0:T(8,128)(2,1)S(1)} %get-tuple-element.12.refs_0_, bf16[128,4096]{1,0:T(8,128)(2,1)S(1)} %get-tuple-element.13.refs_1_, f32[128,768]{1,0:T(8,128)S(1)} %get-tuple-element.14.refs_2_, ...), custom_call_target="tpu_custom_call" | custom-call | tf_op jit(solution)/shard_map/pallas_call | solution.py:858

commit v7 on v6

--- a/solution.py
+++ b/solution.py
@@ -531,24 +531,24 @@
     gq_msg = []
 
     def head(n, inner, grad_keys, grad_values):
+        grad = ctb[:, n * HD : (n + 1) * HD]
+        grad_probs = nt_dot(grad, values)
         q_msg[n].wait_recv()
         mixed = mix[1 + n, :, mycol] + qm_r[n].astype(f32)
         query = (rope(mixed) * scale).astype(bf)
-        grad = ctb[:, n * HD : (n + 1) * HD]
         scores = jnp.where(allowed, nt_dot(query, keys), -1e30)
         top = jnp.max(scores, axis=1, keepdims=True)
         numbers = jnp.where(allowed, jnp.exp(scores - top), 0.0)
-        norm_sum = jnp.sum(numbers, axis=1, keepdims=True)
-        high = numbers.astype(bf)
-        low = (numbers - high.astype(f32)).astype(bf)
-        attn = ((nn_dot(high, values) + nn_dot(low, values)) / norm_sum).astype(bf)
-        at_s[n] = attn
-        delta = jnp.sum(grad.astype(f32) * attn.astype(f32), axis=1, keepdims=True)
-        probs = numbers / norm_sum
-        grad_scores = (probs * (nt_dot(grad, values) - delta)).astype(bf)
+        share = 1.0 / jnp.sum(numbers, axis=1, keepdims=True)
+        probs = numbers * share
+        delta = jnp.sum(probs * grad_probs, axis=1, keepdims=True)
+        grad_scores = (probs * (grad_probs - delta)).astype(bf)
         back = (unrope(nn_dot(grad_scores, keys)) * scale).astype(bf)
         gq[n, x] = back
         gq_msg.append(x_push(gq.at[n, x], gq.at[n, x]))
+        high = numbers.astype(bf)
+        low = (numbers - high.astype(f32)).astype(bf)
+        at_s[n] = ((nn_dot(high, values) + nn_dot(low, values)) * share).astype(bf)
         inner = inner + jnp.sum(back.astype(f32) * mixed, axis=1, keepdims=True)
         grad_keys = grad_keys + tn_dot(grad_scores, query)
         grad_values = grad_values + tn_dot(probs.astype(bf), grad)
@@ -568,8 +568,11 @@
     turn = 1
 
     def terms(q, grads, cc):
-        part = nn_dot(ntr[pl.ds(pl.multiple_of(cc * chips * rows, rows), chips * rows), :], grads)
-        tbuf[q, pl.ds(cc * chips, chips)] = part.astype(bf).reshape(chips, rows, CHUNK)
+        group = chips // 4
+        for r in range(4):
+            first = cc * chips + r * group
+            part = nn_dot(ntr[pl.ds(pl.multiple_of(first * rows, rows), group * rows), :], grads)
+            tbuf[q, pl.ds(first, group)] = part.astype(bf).reshape(group, rows, CHUNK)
 
     def to_side(k, src):
         return rcopy(src, side.at[k], r_send, s_recv.at[k], dev(across(1), y, c, x))
@@ -668,8 +671,20 @@
         gq_msg[n].wait_recv()
         rs_terms(1 + n, jnp.concatenate([gq[n, 0], gq[n, 1]], axis=1))
 
+    send_q(1)
     inner, grad_keys, grad_values = head(0, inner, grad_keys, grad_values)
-    send_q(1)
+    at_msg = [x_push(at_s.at[0, there], at_r.at[0])]
+    block = c * chips + z * SIDE + y
+    cross = c != x
+
+    def to_diag(q):
+        return rcopy(dg_s.at[q], dg_r.at[q], d_send.at[0], d_recv.at[min(q, 1)], d_peer)
+
+    w_copy = rcopy(wbuf.at[0, block], w_own, d_send.at[0], d_recv.at[2], d_peer)
+    gain_copy = rcopy(gbuf.at[:, gcol(block)], gain_own, d_send.at[1], d_recv.at[3], d_peer)
+    gg_copy = rcopy(gg_s, gg_r, d_send.at[1], d_recv.at[4], d_peer)
+    pl.when(cross)(w_copy.start)
+    pl.when(cross)(gain_copy.start)
     rs_head(0)
     inner, grad_keys, grad_values = head(1, inner, grad_keys, grad_values)
     grad_keys = unrope(grad_keys)
@@ -679,18 +694,7 @@
     inner_all = jnp.broadcast_to(inner, (seq, HD))
     in_s[...] = inner_all.T[:8, :]
     in_msg = x_push(in_s, in_r, 2)
-    at_msg = x_push(at_s.at[:, there], at_r)
-    block = c * chips + z * SIDE + y
-    cross = c != x
-
-    def to_diag(q):
-        return rcopy(dg_s.at[q], dg_r.at[q], d_send.at[0], d_recv.at[min(q, 1)], d_peer)
-
-    w_copy = rcopy(wbuf.at[0, block], w_own, d_send.at[0], d_recv.at[2], d_peer)
-    gain_copy = rcopy(gbuf.at[:, gcol(block)], gain_own, d_send.at[1], d_recv.at[3], d_peer)
-    gg_copy = rcopy(gg_s, gg_r, d_send.at[1], d_recv.at[4], d_peer)
-    pl.when(cross)(w_copy.start)
-    pl.when(cross)(gain_copy.start)
+    at_msg.append(x_push(at_s.at[1, there], at_r.at[1]))
     for n in range(half):
         attn_ref[:, pl.ds(pl.multiple_of((x * half + n) * HD, HD), HD)] = at_s[n, here, :]
 
@@ -702,7 +706,6 @@
     keys_sum = gkv_s[:, :HD].astype(f32) + gkv_r[:, :HD].astype(f32)
     values_sum = gkv_s[:, HD:].astype(f32) + gkv_r[:, HD:].astype(f32)
     gkv_all = jnp.concatenate([keys_sum, values_sum], axis=1).astype(bf)
-    rs_terms(0, gkv_all)
     rs_middle(1, [far, 1])
     in_msg.wait_recv()
     inner = inner + jnp.broadcast_to(in_r[:1, :], (HD, seq)).T[:, :1]
@@ -720,6 +723,7 @@
         gi_s[p] = (gain * out * inv[:, :1] - hx[p].astype(f32) * inv_all[:, :1]).astype(bf)
         x_push(gi_s.at[p, there], gi_r.at[p], 0, 1)
     queue = list(range(1, chunks)) + [0]
+    rs_terms(0, gkv_all)
     rs_middle(1, [2])
     rs_sums(0, order)
     rs_middle(1, [0])
@@ -734,8 +738,8 @@
     rs_end(2)
     gg_s[...] = gain_term(sums, gbuf[:, gcol(block)])
     pl.when(cross)(gg_copy.start)
-    at_msg.wait_recv()
     for n in range(half):
+        at_msg[n].wait_recv()
         attn_ref[:, pl.ds(pl.multiple_of(((1 - x) * half + n) * HD, HD), HD)] = at_r[n]
     got_all(gi_r, x_recv.at[1])
     for p in range(PIECES):
@@ -846,7 +850,7 @@
             V((1, rows), f32),
             dma((8,)),
             dma((chunks * SPLIT,)), dma((chunks * SPLIT, chips)), dma((chunks * SPLIT,)),
-            dma((2,)), dma((3,)), dma((12,)),
+            dma((2,)), dma((3,)), dma((13,)),
             dma, dma((chunks, 2)), dma, dma((chunks, nz)), dma((chunks,)), dma((chunks,)),
             dma((2,)), dma((5,)),
         ],

time: 63.9 us -> 63 us (0.986)
  Pallas kernels: 63 us -> 61.6 us
    pallas_call x1, Pallas kernels: 61.8 us -> 60.5 us  [fused(): pl.pallas_call(functools.partial(fused_kernel, n_inter), out_shape=(V((to...]
where the time goes in v7:
time: 63 us; the launch traced here: 62.3 us
  Pallas kernels  61.6 us (98%)
  between operations  0.64 us (1%)
    pallas_call x1, Pallas kernels, fused(): pl.pallas_call(functools.partial(fused_kernel, n_inter), out_shape=(V((to...  60.5 us

profile of v7, /device:TPU:1, one launch (start us, length us, event | category | flops | bytes accessed | tf_op | source)
XLA Modules:
  0.0 62.3 jit_solution(5690832857508726157)
XLA Ops:
  0.6 60.5 %shard_map.93 = (bf16[128,512]{1,0:T(8,128)(2,1)S(1)}, bf16[128,4096]{1,0:T(8,128)(2,1)S(1)}, f32[128,768]{1,0:T(8,128)S(1)}, f32[1,128]{1,0:T(1,128)S(1)}) custom-call(bf16[128,4096]{1,0:T(8,128)(2,1)} %bitcast.6, bf16[1,128]{1,0:T(2,128)(2,1)} %bitcast.8, bf16[128,768]{1,0:T(8,128)(2,1)} %w_ref.1, bf16[128,512]{1,0:T(8,128)(2,1)} %bitcast.7, ...), custom_call_target="tpu_custom_call" | custom-call | tf_op jit(solution)/shard_map/pallas_call | solution.py:804
  61.1 1.2 %shard_map.94 = (bf16[128,512]{1,0:T(8,128)(2,1)}, bf16[128,4096]{1,0:T(8,128)(2,1)}, f32[128,768]{1,0:T(8,128)}, f32[1,128]{1,0:T(1,128)}) custom-call(bf16[128,512]{1,0:T(8,128)(2,1)S(1)} %get-tuple-element.12.refs_0_, bf16[128,4096]{1,0:T(8,128)(2,1)S(1)} %get-tuple-element.13.refs_1_, f32[128,768]{1,0:T(8,128)S(1)} %get-tuple-element.14.refs_2_, ...), custom_call_target="tpu_custom_call" | custom-call | tf_op jit(solution)/shard_map/pallas_call | solution.py:862

commit v8 on v7

--- a/solution.py
+++ b/solution.py
@@ -325,13 +325,6 @@
     def loaded(dst, k):
         pltpu.make_async_copy(dst, dst, ld_sem.at[k]).wait()
 
-    for p in range(PIECES):
-        for b in range(span):
-            j = p * span + b
-            mine = pl.ds(pl.multiple_of((2 * j + x) * rows, rows), rows)
-            other = pl.ds(pl.multiple_of((2 * j + 1 - x) * rows, rows), rows)
-            load(hid_ref.at[:, mine], hx.at[p, here, b * rows : (b + 1) * rows], 0)
-            load(hid_ref.at[:, other], hs.at[p, :, b * rows : (b + 1) * rows], 1)
     load(w_ref.at[:, qcols:], wbuf.at[0, own], 2)
     half = HEADS // 2
     for n in range(half):
@@ -340,6 +333,14 @@
             load(w_ref.at[:, first : first + HD], wbuf.at[1 + n, own, :, xx * HD : (xx + 1) * HD], 2)
     nxt = 3
     load(gain_ref, gain_in, nxt)
+    for p in range(PIECES):
+        for b in range(span):
+            other = pl.ds(pl.multiple_of((2 * (p * span + b) + 1 - x) * rows, rows), rows)
+            load(hid_ref.at[:, other], hs.at[p, :, b * rows : (b + 1) * rows], 1)
+    for p in range(PIECES):
+        for b in range(span):
+            mine = pl.ds(pl.multiple_of((2 * (p * span + b) + x) * rows, rows), rows)
+            load(hid_ref.at[:, mine], hx.at[p, here, b * rows : (b + 1) * rows], 0)
     load(ct_ref.at[:, pl.ds(pl.multiple_of(x * half * HD, HD), half * HD)], ctb.at[here], nxt + 1)
     load(ct_ref.at[:, pl.ds(pl.multiple_of((1 - x) * half * HD, HD), half * HD)], cts, nxt + 2)
     load(cos_hbm, cos_ref, nxt + 3)
@@ -348,8 +349,69 @@
     loaded(gain_in, nxt)
     gcol = lambda g: pl.ds(pl.multiple_of(g * rows, rows), rows)
     gbuf[:, gcol(own)] = gain_in[...].astype(f32)
+    loaded(wbuf.at[:, own], 2)
+    pl.semaphore_wait(barrier, len(peers))
+
+    inner_z = jnp.logical_and(z > 0, z < nz - 1)
+    far = nz - 1
+    steps = chunks * SPLIT
+    spare = steps - 1
+
+    def ag(t, g, device, core=False):
+        part = wbuf.at[t // SPLIT, g, pl.ds(t % SPLIT * (rows // SPLIT), rows // SPLIT)]
+        rs = ag_core.at[t] if core else ag_recv.at[t, g // CORES]
+        return rcopy(part, part, ag_send.at[t], rs, device)
+
+    def arrive(t, g):
+        ag(t, g, x_peer).wait_recv()
+
+    def sent_all(ref, sem):
+        rcopy(ref, ref, sem, d_recv.at[0], x_peer).wait_send()
+
+    def got_all(ref, sem):
+        rcopy(ref, ref, d_send.at[0], sem, x_peer).wait_recv()
+
+    def push(t, g, device, core=False, cond=None):
+        cp = ag(t, g, device, core)
+        if cond is None:
+            cp.start()
+        else:
+            pl.when(cond)(cp.start)
+
+    for n, e in enumerate(plane):
+        rcopy(gbuf.at[:, gcol(own)], gbuf.at[:, gcol(own)], g_sem.at[0], g_sem.at[1],
+              dev(*plane_dev(e), x)).start()
+    ends_z = jnp.logical_not(inner_z)
+
+    def own_z(t, late=False):
+        for d in hops[::-1]:
+            if d == far:
+                cond = inner_z
+            else:
+                cond = (inner_z if late else ends_z) if t >= HELD else None
+            if d != far or not late:
+                push(t, own, dev(across(d), y, c, x), cond=cond)
+
+    def own_y(t):
+        push(t, own, y_peer)
+        push(t, own, c_peer, core=True)
+
+    for t in range(steps):
+        own_z(t)
+        own_y(t)
+    messages = []
+
+    def x_push(src, dst, ss=0, rs=None):
+        if rs is None:
+            rs = len(messages) + 2
+            messages.append(rs)
+        cp = rcopy(src, dst, x_send.at[ss], x_recv.at[rs], x_peer)
+        cp.start()
+        return cp
+
+    loaded(hs, 1)
+    x_push(hs.at[0], hx.at[0, here], 0, 0)
     loaded(hx.at[:, here], 0)
-    loaded(hs, 1)
     total = jnp.zeros((toks, 1), f32)
     for p in range(PIECES):
         a = hx[p, here, :].astype(f32)
@@ -358,70 +420,10 @@
     inv = jnp.broadcast_to(lax.rsqrt(total / width + eps_norm), (toks, HD))
     inv_all[here, :] = inv
     inv_s[...] = inv.T[:8, :]
-    loaded(wbuf.at[:, own], 2)
+    inv_msg = x_push(inv_s, inv_r, 1)
+    for p in range(1, PIECES):
+        x_push(hs.at[p], hx.at[p, here], 0, 0)
     loaded(cts, nxt + 2)
-    pl.semaphore_wait(barrier, len(peers))
-
-    inner_z = jnp.logical_and(z > 0, z < nz - 1)
-    far = nz - 1
-    steps = chunks * SPLIT
-    spare = steps - 1
-
-    def ag(t, g, device, core=False):
-        part = wbuf.at[t // SPLIT, g, pl.ds(t % SPLIT * (rows // SPLIT), rows // SPLIT)]
-        rs = ag_core.at[t] if core else ag_recv.at[t, g // CORES]
-        return rcopy(part, part, ag_send.at[t], rs, device)
-
-    def arrive(t, g):
-        ag(t, g, x_peer).wait_recv()
-
-    def sent_all(ref, sem):
-        rcopy(ref, ref, sem, d_recv.at[0], x_peer).wait_send()
-
-    def got_all(ref, sem):
-        rcopy(ref, ref, d_send.at[0], sem, x_peer).wait_recv()
-
-    def push(t, g, device, core=False, cond=None):
-        cp = ag(t, g, device, core)
-        if cond is None:
-            cp.start()
-        else:
-            pl.when(cond)(cp.start)
-
-    for n, e in enumerate(plane):
-        rcopy(gbuf.at[:, gcol(own)], gbuf.at[:, gcol(own)], g_sem.at[0], g_sem.at[1],
-              dev(*plane_dev(e), x)).start()
-    ends_z = jnp.logical_not(inner_z)
-
-    def own_z(t, late=False):
-        for d in hops[::-1]:
-            if d == far:
-                cond = inner_z
-            else:
-                cond = (inner_z if late else ends_z) if t >= HELD else None
-            if d != far or not late:
-                push(t, own, dev(across(d), y, c, x), cond=cond)
-
-    def own_y(t):
-        push(t, own, y_peer)
-        push(t, own, c_peer, core=True)
-
-    for t in range(steps):
-        own_z(t)
-        own_y(t)
-    messages = []
-
-    def x_push(src, dst, ss=0, rs=None):
-        if rs is None:
-            rs = len(messages) + 2
-            messages.append(rs)
-        cp = rcopy(src, dst, x_send.at[ss], x_recv.at[rs], x_peer)
-        cp.start()
-        return cp
-
-    inv_msg = x_push(inv_s, inv_r, 1)
-    for p in range(PIECES):
-        x_push(hs.at[p], hx.at[p, here], 0, 0)
     ct_msg = x_push(cts, ctb.at[here])
 
     def near(n):

time: 63 us -> 63 us (level)
  no operation moved by 1% of the time
where the time goes in v8:
time: 63 us; the launch traced here: 62.3 us
  Pallas kernels  61.6 us (98%)
  between operations  0.64 us (1%)
    pallas_call x1, Pallas kernels, fused(): pl.pallas_call(functools.partial(fused_kernel, n_inter), out_shape=(V((to...  60.5 us

profile of v8, /device:TPU:1, one launch (start us, length us, event | category | flops | bytes accessed | tf_op | source)
XLA Modules:
  0.0 62.3 jit_solution(6516068728726214030)
XLA Ops:
  0.6 60.5 %shard_map.93 = (bf16[128,512]{1,0:T(8,128)(2,1)S(1)}, bf16[128,4096]{1,0:T(8,128)(2,1)S(1)}, f32[128,768]{1,0:T(8,128)S(1)}, f32[1,128]{1,0:T(1,128)S(1)}) custom-call(bf16[128,4096]{1,0:T(8,128)(2,1)} %bitcast.6, bf16[1,128]{1,0:T(2,128)(2,1)} %bitcast.8, bf16[128,768]{1,0:T(8,128)(2,1)} %w_ref.1, bf16[128,512]{1,0:T(8,128)(2,1)} %bitcast.7, ...), custom_call_target="tpu_custom_call" | custom-call | tf_op jit(solution)/shard_map/pallas_call | solution.py:806
  61.1 1.2 %shard_map.94 = (bf16[128,512]{1,0:T(8,128)(2,1)}, bf16[128,4096]{1,0:T(8,128)(2,1)}, f32[128,768]{1,0:T(8,128)}, f32[1,128]{1,0:T(1,128)}) custom-call(bf16[128,512]{1,0:T(8,128)(2,1)S(1)} %get-tuple-element.12.refs_0_, bf16[128,4096]{1,0:T(8,128)(2,1)S(1)} %get-tuple-element.13.refs_1_, f32[128,768]{1,0:T(8,128)S(1)} %get-tuple-element.14.refs_2_, ...), custom_call_target="tpu_custom_call" | custom-call | tf_op jit(solution)/shard_map/pallas_call | solution.py:864
